TPU v7x, 512 devices: a whole 4x8x8 slice. The times are simulated.
512 devices in a mesh: ep: 64 (over z, y_hi, core), edp: 8 (over y_lo, x).
Axes of the slice: x: 4, y: 8 (y_hi: 4, y_lo: 2; y = y_hi * 2 + y_lo), z: 8, core: 2. Of those that a mesh axis runs over, the one named last changes fastest.
Arguments:
- expert_grads: bfloat16 [64, 8, 32, 7168], P('ep', 'edp'), may hold values from -1.59375 to 1.59375
- expert_param: float32 [64, 32, 7168], P('ep', 'edp'), may hold values from -3 to 3
- expert_moment: float32 [64, 32, 7168], P('ep', 'edp'), may hold values from -1.2 to 1.2
- expert_second: float32 [64, 32, 7168], P('ep', 'edp'), may hold values from 0.01 to 1
- dense_grads: bfloat16 [64, 8, 64, 7168], P('ep', 'edp'), may hold values from -1.59375 to 1.59375
- dense_param: float32 [458752], P(('ep', 'edp')), may hold values from -3 to 3
- dense_moment: float32 [458752], P(('ep', 'edp')), may hold values from -1.2 to 1.2
- dense_second: float32 [458752], P(('ep', 'edp')), may hold values from 0.01 to 1
- writer: int32 [64, 8, 1], P('ep', 'edp'), may hold values from 0 to 7; in each aligned block of 8 rows (0 to 7, 8 to 15, ..., all dimensions but the last counted through in order) at most 4 rows name the same one
- live_blocks: int32 [64, 8], P('ep', 'edp'), may hold values from 1 to 224
Outputs:
- expert_param_out: float32 [64, 32, 7168], P('ep', 'edp')
- expert_moment_out: float32 [64, 32, 7168], P('ep', 'edp')
- expert_second_out: float32 [64, 32, 7168], P('ep', 'edp')
- dense_param_out: float32 [458752], P(('ep', 'edp'))
- dense_moment_out: float32 [458752], P(('ep', 'edp'))
- dense_second_out: float32 [458752], P(('ep', 'edp'))
- save_slots: bfloat16 [64, 8, 4, 28672], P('ep', 'edp')
Inputs may be any that keep to these rules, and one draw needn't show every extreme that they name: `writer`: within one expert no rank stores more than 4 slices, and in some experts one rank stores exactly 4.
All inputs are finite; a program needn't handle non-finite values.
Results may differ from a plain program's by a relative error of at most 0.013.
Values may be sent and summed in bfloat16 or wider, within the bound.
No kernel may reach another device: no remote copies, remote signals or barrier semaphores. Data moves between devices by JAX's collectives and lax.ppermute only.
A program may use at most 64 MiB of HBM per device.

v0:
```python
import jax
import jax.numpy as jnp
from jax import lax
from jax.sharding import PartitionSpec as P

BETA_FIRST = 0.9
BETA_SECOND = 0.95
LEARN_RATE = 0.01
DECAY_RATE = 0.1
EPSILON = 1e-08
FIRST_BIAS = 1.0 - BETA_FIRST**10
SECOND_BIAS = 1.0 - BETA_SECOND**10


def in_blocks(x, dim, length):
    before, after = (x.shape[:dim], x.shape[dim + 1 :])
    return jnp.moveaxis(x.reshape(*before, length, -1, *after), dim, 0)


def sum_at_owner(x, axis, dim):
    tiles = in_blocks(x, dim, lax.axis_size(axis))
    arrived = lax.all_to_all(tiles, axis, split_axis=0, concat_axis=0, tiled=True)
    return arrived.astype(jnp.float32).sum(axis=0)


def sent_and_summed(x, axis, dim):
    tiles = in_blocks(x, dim, lax.axis_size(axis))
    arrived = lax.all_to_all(tiles, axis, split_axis=0, concat_axis=0, tiled=True)
    return arrived.sum(axis=0)


def adam_update(master, moment, second, gradient):
    moment_new = BETA_FIRST * moment + (1.0 - BETA_FIRST) * gradient
    second_new = BETA_SECOND * second + (1.0 - BETA_SECOND) * gradient * gradient
    direction = moment_new / FIRST_BIAS / (jnp.sqrt(second_new / SECOND_BIAS) + EPSILON)
    master_new = master - LEARN_RATE * (direction + DECAY_RATE * master)
    return (master_new, moment_new, second_new)


def body(
    expert_grads,
    expert_param,
    expert_moment,
    expert_second,
    dense_grads,
    dense_param,
    dense_moment,
    dense_second,
    writer,
    live_blocks,
):
    replicas = lax.axis_size("edp")
    groups = lax.axis_size("ep")
    local_grad = expert_grads[0, 0].astype(jnp.float32)
    expert_sum = sum_at_owner(local_grad.astype(jnp.bfloat16), "edp", 0)
    dense_local = dense_grads[0, 0].astype(jnp.float32).reshape(-1)
    shaped = dense_local.reshape(groups, replicas, -1)
    partial_sum = sum_at_owner(shaped.astype(jnp.bfloat16), "edp", 1)
    dense_sum = sent_and_summed(partial_sum, "ep", 0).reshape(-1)
    expert_new, expert_mom, expert_sec = adam_update(
        expert_param[0], expert_moment[0], expert_second[0], expert_sum
    )
    dense_new, dense_mom, dense_sec = adam_update(
        dense_param, dense_moment, dense_second, dense_sum
    )
    flat_slice = expert_new.astype(jnp.bfloat16).reshape(-1)
    positions = lax.broadcasted_iota(jnp.int32, flat_slice.shape, 0) // 128
    kept_slice = jnp.where(positions < live_blocks[0, 0], flat_slice, jnp.zeros_like(flat_slice))
    target = writer[0, 0, 0]
    slot_count = max(2, replicas // 2)
    rank_ids = lax.broadcasted_iota(jnp.int32, (replicas, 1), 0)
    chosen = rank_ids == target
    outgoing = jnp.where(chosen, kept_slice[None, :], jnp.zeros_like(kept_slice)[None, :])
    present = chosen.astype(jnp.bfloat16)
    received, arrived = (
        lax.all_to_all(outgoing, "edp", split_axis=0, concat_axis=0, tiled=True),
        lax.all_to_all(present, "edp", split_axis=0, concat_axis=0, tiled=True),
    )
    arrived_flag = arrived[:, 0].astype(jnp.float32)
    before = jnp.cumsum(arrived_flag) - arrived_flag
    slot_ids = lax.broadcasted_iota(jnp.int32, (slot_count, replicas), 0).astype(jnp.float32)
    selector = jnp.where(
        (slot_ids == before[None, :]) & (arrived_flag[None, :] > 0.5), 1.0, 0.0
    ).astype(jnp.bfloat16)
    saved_slots = jnp.dot(selector, received, preferred_element_type=jnp.float32).astype(
        jnp.bfloat16
    )
    return (
        expert_new[None],
        expert_mom[None],
        expert_sec[None],
        dense_new,
        dense_mom,
        dense_sec,
        saved_slots[None, None],
    )


def solution(mesh):
    placed = (
        P("ep", "edp", None, None),
        P("ep", "edp", None),
        P("ep", "edp", None),
        P("ep", "edp", None),
        P("ep", "edp", None, None),
        P(("ep", "edp")),
        P(("ep", "edp")),
        P(("ep", "edp")),
        P("ep", "edp", None),
        P("ep", "edp"),
    )
    return jax.shard_map(
        body,
        mesh=mesh,
        in_specs=placed,
        out_specs=(
            P("ep", "edp", None),
            P("ep", "edp", None),
            P("ep", "edp", None),
            P(("ep", "edp")),
            P(("ep", "edp")),
            P(("ep", "edp")),
            P("ep", "edp", None, None),
        ),
        check_vma=False,
    )
```

profile of v0, /device:TPU:1, one launch (start us, length us, event | category | flops | bytes accessed | tf_op | source)
XLA Modules:
  0.0 87.3 jit_solution(15545467351799687173)
XLA Ops:
  0.7 2.0 %reshape.223 = bf16[8,4,7168]{2,1,0:T(4,128)(2,1)} reshape(bf16[1,1,32,7168]{3,2,1,0:T(8,128)(2,1)} %param.10) | data formatting | bytes 917504 | tf_op jit(solution)/shard_map/reshape | solution.py:17
  2.7 5.9 %all-to-all-start = ((bf16[8,4,7168]{2,1,0:T(4,128)(2,1)}), bf16[8,4,7168]{2,1,0:T(4,128)(2,1)S(1)}, u32[]{:S(2)}, u32[]{:S(2)}) async-start(bf16[8,4,7168]{2,1,0:T(4,128)(2,1)} %reshape.223), calls=%async_computation | async-start | bytes 917504 | tf_op jit(solution)/shard_map/all_to_all | solution.py:22
  10.1 1.1 %copy.17 = bf16[8,64,1,896]{3,1,2,0:T(8,128)(2,1)} copy(bf16[8,64,1,896]{3,0,1,2:T(8,128)(2,1)S(1)} %bitcast.40) | data formatting | bytes 1835008 | tf_op jit(solution)/shard_map/transpose | solution.py:17
  11.1 0.6 compare_convert_fusion
  11.7 3.7 %all-to-all-done = bf16[8,4,7168]{2,1,0:T(4,128)(2,1)S(1)} async-done(((bf16[8,4,7168]{2,1,0:T(4,128)(2,1)}), bf16[8,4,7168]{2,1,0:T(4,128)(2,1)S(1)}, u32[]{:S(2)}, u32[]{:S(2)}) %all-to-all-start) | async-done | bytes 458784 | tf_op jit(solution)/shard_map/all_to_all | solution.py:22
  15.4 3.3 %all-to-all-start.3 = ((bf16[8,1,1]{2,1,0:T(2,128)(2,1)}), bf16[8,1,1]{2,1,0:T(2,128)(2,1)S(1)}, u32[]{:S(2)}, u32[]{:S(2)}) async-start(bf16[8,1,1]{2,1,0:T(2,128)(2,1)} %compare_convert_fusion), calls=%async_computation.3 | async-start | bytes 8192 | tf_op jit(solution)/shard_map/all_to_all | solution.py:77
  18.7 0.2 convert_reduce_fusion.1
  19.0 0.9 %multiply_subtract_fusion = (f32[1,4,7168]{2,1,0:T(4,128)}, f32[1,4,7168]{2,1,0:T(4,128)}, f32[1,4,7168]{2,1,0:T(4,128)}, f32[1,56,4,128]{3,2,1,0:T(4,128)S(1)}, f32[1,56,4,128]{3,2,1,0:T(4,128)S(1)}) fusion(f32[1,4,7168]{2,1,0:T(4,128)S(1)} %copy-done.1, f32[4,7168]{1,0:T(4,128)S(1)} %convert_reduce_fusion.1, f32[1,4,7168]{2,1,0:T(4,128)S(1)} %copy-done.2, ...), kind=kLoop, calls=%fused_computation.26 | loop fusion | flops 430080 | bytes 1032192 | tf_op jit(solution)/shard_map/sub | solution.py:36
  20.0 3.6 %all-to-all-done.3 = bf16[8,1,1]{2,1,0:T(2,128)(2,1)S(1)} async-done(((bf16[8,1,1]{2,1,0:T(2,128)(2,1)}), bf16[8,1,1]{2,1,0:T(2,128)(2,1)S(1)}, u32[]{:S(2)}, u32[]{:S(2)}) %all-to-all-start.3) | async-done | bytes 48 | tf_op jit(solution)/shard_map/all_to_all | solution.py:77
  23.6 3.6 %all-to-all-start.1 = ((bf16[8,64,1,896]{3,1,2,0:T(8,128)(2,1)}), bf16[8,64,1,896]{3,1,2,0:T(8,128)(2,1)S(1)}, u32[]{:S(2)}, u32[]{:S(2)}) async-start(bf16[8,64,1,896]{3,1,2,0:T(8,128)(2,1)} %copy.17), calls=%async_computation.1 | async-start | bytes 1835008 | tf_op jit(solution)/shard_map/all_to_all | solution.py:22
  27.2 0.8 broadcast_select_fusion
  28.0 0.5 broadcast.206
  28.5 3.4 %reduce.5 = bf16[8,28672]{1,0:T(8,128)(2,1)S(1)} reduce(bf16[8,1,28672]{2,1,0:T(2,128)(2,1)S(1)} %broadcast_select_fusion, bf16[]{:T(256)} %broadcast.206), dimensions={1}, to_apply=%broadcast_select_fusion.reduce_sub_computation | reduce | bytes 917506 | tf_op jit(solution)/shard_map/jit(_where)/select_n | solution.py:73
  31.9 1.1 %reshape.230 = bf16[8,2,14336]{2,1,0:T(2,128)(2,1)} reshape(bf16[8,28672]{1,0:T(8,128)(2,1)S(1)} %reduce.5) | data formatting | bytes 917504
  33.0 2.9 %all-to-all-done.1 = bf16[8,64,1,896]{3,1,2,0:T(8,128)(2,1)S(1)} async-done(((bf16[8,64,1,896]{3,1,2,0:T(8,128)(2,1)}), bf16[8,64,1,896]{3,1,2,0:T(8,128)(2,1)S(1)}, u32[]{:S(2)}, u32[]{:S(2)}) %all-to-all-start.1) | async-done | bytes 917536 | tf_op jit(solution)/shard_map/all_to_all | solution.py:22
  36.0 3.5 %all-to-all-start.4 = ((bf16[8,2,14336]{2,1,0:T(2,128)(2,1)}), bf16[8,2,14336]{2,1,0:T(2,128)(2,1)S(1)}, u32[]{:S(2)}, u32[]{:S(2)}) async-start(bf16[8,2,14336]{2,1,0:T(2,128)(2,1)} %reshape.230), calls=%async_computation.4 | async-start | bytes 917504 | tf_op jit(solution)/shard_map/all_to_all | solution.py:76
  39.7 0.8 reshape.224
  40.6 5.7 %all-to-all-done.4 = bf16[8,2,14336]{2,1,0:T(2,128)(2,1)S(1)} async-done(((bf16[8,2,14336]{2,1,0:T(2,128)(2,1)}), bf16[8,2,14336]{2,1,0:T(2,128)(2,1)S(1)}, u32[]{:S(2)}, u32[]{:S(2)}) %all-to-all-start.4) | async-done | bytes 458784 | tf_op jit(solution)/shard_map/all_to_all | solution.py:76
  46.2 25.2 %all-to-all-start.2 = ((f32[64,1,1,896]{3,2,1,0:T(1,128)}), f32[64,1,1,896]{3,2,1,0:T(1,128)S(1)}, u32[]{:S(2)}, u32[]{:S(2)}) async-start(f32[64,1,1,896]{3,2,1,0:T(1,128)} %reshape.224), calls=%async_computation.2 | async-start | bytes 458752 | tf_op jit(solution)/shard_map/all_to_all | solution.py:28
  71.5 0.2 reduce-window.8
  71.7 0.5 reshape.231
  72.2 1.3 %fusion = bf16[1,1,4,28672]{3,2,1,0:T(4,128)(2,1)} fusion(bf16[8,1,28672]{2,1,0:T(2,128)(2,1)S(1)} %reshape.231, f32[8]{0:T(128)S(1)} %bitcast_subtract_fusion, pred[8]{0:T(512)(128)(4,1)S(1)} %broadcast_compare_fusion, f32[4]{0:T(128)S(1)} %iota_convert_fusion), kind=kOutput, calls=%fused_computation.1 | convolution fusion | flops 1949824 | bytes 688184 | tf_op jit(solution)/shard_map/dot_general | solution.py:85
  73.5 13.0 %all-to-all-done.2 = f32[64,1,1,896]{3,2,1,0:T(1,128)S(1)} async-done(((f32[64,1,1,896]{3,2,1,0:T(1,128)}), f32[64,1,1,896]{3,2,1,0:T(1,128)S(1)}, u32[]{:S(2)}, u32[]{:S(2)}) %all-to-all-start.2) | async-done | bytes 229408 | tf_op jit(solution)/shard_map/all_to_all | solution.py:28
  86.7 0.6 multiply_subtract_fusion.1
  (27 shorter events, 0.8 us)
Async XLA Ops:
  0.6 9.2 %copy-start.1 = (f32[1,4,7168]{2,1,0:T(4,128)S(1)}, f32[1,4,7168]{2,1,0:T(4,128)}, u32[]{:S(2)}) copy-start(f32[1,4,7168]{2,1,0:T(4,128)} %param.11) | copy-start | bytes 344068
  0.6 9.2 %copy-start = (bf16[1,1,64,7168]{3,2,1,0:T(8,128)(2,1)S(1)}, bf16[1,1,64,7168]{3,2,1,0:T(8,128)(2,1)}, u32[]{:S(2)}) copy-start(bf16[1,1,64,7168]{3,2,1,0:T(8,128)(2,1)} %param.14) | copy-start | bytes 2752516
  2.7 12.7 %all-to-all-start = ((bf16[8,4,7168]{2,1,0:T(4,128)(2,1)}), bf16[8,4,7168]{2,1,0:T(4,128)(2,1)S(1)}, u32[]{:S(2)}, u32[]{:S(2)}) async-start(bf16[8,4,7168]{2,1,0:T(4,128)(2,1)} %reshape.223), calls=%async_computation | async-start | bytes 917504 | tf_op jit(solution)/shard_map/all_to_all | solution.py:22
  10.0 8.9 %copy-start.2 = (f32[1,4,7168]{2,1,0:T(4,128)S(1)}, f32[1,4,7168]{2,1,0:T(4,128)}, u32[]{:S(2)}) copy-start(f32[1,4,7168]{2,1,0:T(4,128)} %param.12) | copy-start | bytes 344068
  10.0 8.9 %copy-start.3 = (f32[1,4,7168]{2,1,0:T(4,128)S(1)}, f32[1,4,7168]{2,1,0:T(4,128)}, u32[]{:S(2)}) copy-start(f32[1,4,7168]{2,1,0:T(4,128)} %param.13) | copy-start | bytes 344068
  15.4 8.2 %all-to-all-start.3 = ((bf16[8,1,1]{2,1,0:T(2,128)(2,1)}), bf16[8,1,1]{2,1,0:T(2,128)(2,1)S(1)}, u32[]{:S(2)}, u32[]{:S(2)}) async-start(bf16[8,1,1]{2,1,0:T(2,128)(2,1)} %compare_convert_fusion), calls=%async_computation.3 | async-start | bytes 8192 | tf_op jit(solution)/shard_map/all_to_all | solution.py:77
  23.6 12.3 %all-to-all-start.1 = ((bf16[8,64,1,896]{3,1,2,0:T(8,128)(2,1)}), bf16[8,64,1,896]{3,1,2,0:T(8,128)(2,1)S(1)}, u32[]{:S(2)}, u32[]{:S(2)}) async-start(bf16[8,64,1,896]{3,1,2,0:T(8,128)(2,1)} %copy.17), calls=%async_computation.1 | async-start | bytes 1835008 | tf_op jit(solution)/shard_map/all_to_all | solution.py:22
  36.0 10.3 %all-to-all-start.4 = ((bf16[8,2,14336]{2,1,0:T(2,128)(2,1)}), bf16[8,2,14336]{2,1,0:T(2,128)(2,1)S(1)}, u32[]{:S(2)}, u32[]{:S(2)}) async-start(bf16[8,2,14336]{2,1,0:T(2,128)(2,1)} %reshape.230), calls=%async_computation.4 | async-start | bytes 917504 | tf_op jit(solution)/shard_map/all_to_all | solution.py:76
  46.2 40.2 %all-to-all-start.2 = ((f32[64,1,1,896]{3,2,1,0:T(1,128)}), f32[64,1,1,896]{3,2,1,0:T(1,128)S(1)}, u32[]{:S(2)}, u32[]{:S(2)}) async-start(f32[64,1,1,896]{3,2,1,0:T(1,128)} %reshape.224), calls=%async_computation.2 | async-start | bytes 458752 | tf_op jit(solution)/shard_map/all_to_all | solution.py:28
  71.7 15.0 %copy-start.4 = (f32[896]{0:T(1024)S(1)}, f32[896]{0:T(1024)}, u32[]{:S(2)}) copy-start(f32[896]{0:T(1024)} %param.15) | copy-start | bytes 10756
  71.7 15.0 %copy-start.5 = (f32[896]{0:T(1024)S(1)}, f32[896]{0:T(1024)}, u32[]{:S(2)}) copy-start(f32[896]{0:T(1024)} %param.16) | copy-start | bytes 10756
  71.7 15.0 %copy-start.6 = (f32[896]{0:T(1024)S(1)}, f32[896]{0:T(1024)}, u32[]{:S(2)}) copy-start(f32[896]{0:T(1024)} %param.17) | copy-start | bytes 10756
where the time goes:
time: 87.8 us; the launch traced here: 87.3 us
  starting transfers between devices  41.4 us (47%)
  waiting for transfers between devices  28.9 us (33%)
  other arithmetic  7.29 us (8%)
  local copies, waits for them, and re-layouts  6.25 us (7%)
  between operations  2.14 us (2%)
  matrix products  1.3 us (1%)
    all_to_all x1, starting transfers between devices, sent_and_summed(): lax.all_to_all(tiles, axis, split_axis=0, concat_axis=0, tiled=True)  25.2 us
    all_to_all x1, waiting for transfers between devices, sent_and_summed(): lax.all_to_all(tiles, axis, split_axis=0, concat_axis=0, tiled=True)  13 us
    all_to_all x2, starting transfers between devices, sum_at_owner(): lax.all_to_all(tiles, axis, split_axis=0, concat_axis=0, tiled=True)  9.4 us
    all_to_all x2, waiting for transfers between devices, sum_at_owner(): lax.all_to_all(tiles, axis, split_axis=0, concat_axis=0, tiled=True)  6.61 us
    all_to_all x1, waiting for transfers between devices, body(): lax.all_to_all(outgoing, 'edp', split_axis=0, concat_axis=0, tiled=True)  5.68 us
    select_n x2, other arithmetic, body(): jnp.where(chosen, kept_slice[None, :], jnp.zeros_like(kept_slice)[None, :])  4.24 us
    all_to_all x1, waiting for transfers between devices, body(): lax.all_to_all(present, 'edp', split_axis=0, concat_axis=0, tiled=True)  3.62 us
    all_to_all x1, starting transfers between devices, body(): lax.all_to_all(outgoing, 'edp', split_axis=0, concat_axis=0, tiled=True)  3.47 us
  transfers between devices with their start and end apart: 5, of which 5 were waited for; matrix products, arithmetic and copies ran while one was open for 14% of the time, Pallas kernels for 0%

commit v1 on v0

v1 whole, which is shorter than its diff:
```python
import jax
import jax.numpy as jnp
from jax import lax
from jax.sharding import Mesh, PartitionSpec as P

BETA_FIRST = 0.9
BETA_SECOND = 0.95
LEARN_RATE = 0.01
DECAY_RATE = 0.1
EPSILON = 1e-08
FIRST_BIAS = 1.0 - BETA_FIRST**10
SECOND_BIAS = 1.0 - BETA_SECOND**10
EP = ("z", "yh", "c")
EDP = ("yl", "x")
ABSENT = 2.0**100


def adam_update(master, moment, second, gradient):
    moment_new = BETA_FIRST * moment + (1.0 - BETA_FIRST) * gradient
    second_new = BETA_SECOND * second + (1.0 - BETA_SECOND) * gradient * gradient
    direction = moment_new / FIRST_BIAS / (jnp.sqrt(second_new / SECOND_BIAS) + EPSILON)
    master_new = master - LEARN_RATE * (direction + DECAY_RATE * master)
    return (master_new, moment_new, second_new)


def to_tiles(x):
    return x.reshape(4, 56, 128).transpose(1, 0, 2).reshape(224, 128)


def from_tiles(x):
    return x.reshape(56, 4, 128).transpose(1, 0, 2).reshape(4, 7168)


def body(
    expert_grads,
    expert_param,
    expert_moment,
    expert_second,
    dense_grads,
    dense_param,
    dense_moment,
    dense_second,
    writer,
    live_blocks,
):
    expert_part = expert_grads[0, 0].reshape(8, 4, 56, 128).transpose(0, 2, 1, 3)
    expert_part = expert_part.reshape(8, 224, 128)
    dense_part = dense_grads[0, 0].reshape(8, 8, 8, 7, 128).transpose(2, 0, 3, 1, 4)
    dense_part = dense_part.reshape(8, 448, 128)
    outgoing = jnp.concatenate([expert_part, dense_part], axis=1)
    arrived = lax.all_to_all(outgoing, EDP, split_axis=0, concat_axis=0, tiled=True)
    expert_sum = arrived[:, :224].astype(jnp.float32).sum(axis=0)
    dense_partial = arrived[:, 224:].astype(jnp.float32).sum(axis=0)

    expert_new, expert_mom, expert_sec = adam_update(
        to_tiles(expert_param[0]), to_tiles(expert_moment[0]), to_tiles(expert_second[0]), expert_sum
    )
    row = lax.broadcasted_iota(jnp.int32, (224, 128), 0)
    block = (row % 4) * 56 + row // 4
    kept = jnp.where(block < live_blocks[0, 0], expert_new, 0.0).astype(jnp.bfloat16)
    rank = lax.broadcasted_iota(jnp.int32, (8, 224, 128), 0)
    slices = jnp.where(rank == writer[0, 0, 0], kept[None], jnp.bfloat16(ABSENT))
    received = lax.all_to_all(slices, EDP, split_axis=0, concat_axis=0, tiled=True)

    core = lax.axis_index("c")
    rows = dense_partial.reshape(8, 7, 8, 128).transpose(0, 2, 1, 3).reshape(32, 2, 7, 128)
    mine = jnp.where(core == 0, rows[:, 0], rows[:, 1])
    other = jnp.where(core == 0, rows[:, 1], rows[:, 0])
    swapped = lax.ppermute(other, "c", [(0, 1), (1, 0)])
    pair = jnp.pad(mine + swapped, ((0, 0), (0, 1), (0, 0)))
    dense_arrived = lax.all_to_all(pair, ("z", "yh"), split_axis=0, concat_axis=0, tiled=True)
    dense_sum = dense_arrived.sum(axis=0)[:7].reshape(-1)

    present = (received[:, 0, 0].astype(jnp.float32) < ABSENT / 2)
    index = lax.broadcasted_iota(jnp.int32, (8, 8), 0)
    index2 = lax.broadcasted_iota(jnp.int32, (8, 8), 1)
    before = jnp.sum(jnp.where((index2 < index) & present[None, :], 1, 0), axis=1)
    slot = lax.broadcasted_iota(jnp.int32, (4, 8), 0)
    selector = ((slot == before[None, :]) & present[None, :]).astype(jnp.bfloat16)
    clean = jnp.where(present[:, None, None], received, jnp.bfloat16(0))
    saved = jnp.einsum("kr,rql->kql", selector, clean, preferred_element_type=jnp.float32)
    saved = saved.astype(jnp.bfloat16).reshape(4, 56, 4, 128).transpose(0, 2, 1, 3).reshape(4, 28672)

    dense_new, dense_mom, dense_sec = adam_update(
        dense_param, dense_moment, dense_second, dense_sum
    )
    return (
        from_tiles(expert_new)[None],
        from_tiles(expert_mom)[None],
        from_tiles(expert_sec)[None],
        dense_new,
        dense_mom,
        dense_sec,
        saved[None, None],
    )


def solution(mesh):
    fine = Mesh(mesh.devices.reshape(8, 4, 2, 2, 4), EP + EDP)
    state = P(EP, EDP, None)
    flat = P(EP + EDP)
    return jax.shard_map(
        body,
        mesh=fine,
        in_specs=(
            P(EP, EDP, None, None),
            state,
            state,
            state,
            P(EP, EDP, None, None),
            flat,
            flat,
            flat,
            state,
            P(EP, EDP),
        ),
        out_specs=(state, state, state, flat, flat, flat, P(EP, EDP, None, None)),
        check_vma=False,
    )
```

time: 87.8 us -> 74.5 us (0.85)
  the two profiles are of different devices: /device:TPU:1 before, /device:TPU:8 now
where the time goes in v1:
time: 74.5 us; the launch traced here: 74.1 us
  starting transfers between devices  30.7 us (41%)
  waiting for transfers between devices  30.7 us (41%)
  local copies, waits for them, and re-layouts  5.36 us (7%)
  other arithmetic  4.85 us (7%)
  between operations  2.17 us (3%)
    all_to_all x1, starting transfers between devices, body(): lax.all_to_all(pair, ('z', 'yh'), split_axis=0, concat_axis=0, tiled=True)  15.1 us
    all_to_all x1, waiting for transfers between devices, body(): lax.all_to_all(outgoing, EDP, split_axis=0, concat_axis=0, tiled=True)  12.8 us
    all_to_all x1, waiting for transfers between devices, body(): lax.all_to_all(pair, ('z', 'yh'), split_axis=0, concat_axis=0, tiled=True)  11.4 us
    all_to_all x1, starting transfers between devices, body(): lax.all_to_all(outgoing, EDP, split_axis=0, concat_axis=0, tiled=True)  9.42 us
    all_to_all x1, waiting for transfers between devices, body(): lax.all_to_all(slices, EDP, split_axis=0, concat_axis=0, tiled=True)  5.31 us
    all_to_all x1, starting transfers between devices, body(): lax.all_to_all(slices, EDP, split_axis=0, concat_axis=0, tiled=True)  4.26 us
    another operation x1, local copies, waits for them, and re-layouts, body(): dense_grads[0, 0].reshape(8, 8, 8, 7, 128).transpose(2, 0, 3, 1, 4)  2.36 us
    ppermute x1, starting transfers between devices, body(): swapped = lax.ppermute(other, 'c', [(0, 1), (1, 0)])  1.92 us
  transfers between devices with their start and end apart: 4, of which 4 were waited for; matrix products, arithmetic and copies ran while one was open for 4% of the time, Pallas kernels for 0%

profile of v1, /device:TPU:8, one launch (start us, length us, event | category | flops | bytes accessed | tf_op | source)
XLA Modules:
  0.0 74.1 jit_solution(16704771204790624135)
XLA Ops:
  0.6 2.4 %reshape_squeeze.13 = bf16[8,8,8,7,128]{4,3,2,1,0:T(8,128)(2,1)S(1)} reshape(bf16[1,1,64,7168]{3,2,1,0:T(8,128)(2,1)} %param.14) | data formatting | bytes 1835008 | tf_op jit(solution)/shard_map/reshape;squeeze | solution.py:48
  3.0 1.1 %copy.62 = bf16[8,8,7,8,128]{4,3,2,1,0:T(8,128)(2,1)S(1)} copy(bf16[8,8,7,8,128]{4,2,0,3,1:T(8,128)(2,1)S(1)} %bitcast.90) | data formatting | bytes 1835008 | tf_op jit(solution)/shard_map/transpose | solution.py:48
  4.2 0.2 copy.61
  4.4 1.2 %pad_maximum_fusion = bf16[8,672,128]{2,1,0:T(8,128)(2,1)} fusion(bf16[8,448,128]{2,1,0:T(8,128)(2,1)S(1)} %bitcast.91, bf16[8,224,128]{2,1,0:T(8,128)(2,1)S(1)} %copy.63), kind=kLoop, calls=%fused_computation.1 | loop fusion | flops 2752512 | bytes 2752512 | tf_op jit(solution)/shard_map/concatenate | solution.py:50
  5.6 9.4 %all-to-all-start = ((bf16[8,672,128]{2,1,0:T(8,128)(2,1)}), bf16[8,672,128]{2,1,0:T(8,128)(2,1)S(1)}, u32[]{:S(2)}, u32[]{:S(2)}) async-start(bf16[8,672,128]{2,1,0:T(8,128)(2,1)} %pad_maximum_fusion), calls=%async_computation | async-start | bytes 2752512 | tf_op jit(solution)/shard_map/all_to_all | solution.py:51
  16.5 12.8 %all-to-all-done = bf16[8,672,128]{2,1,0:T(8,128)(2,1)S(1)} async-done(((bf16[8,672,128]{2,1,0:T(8,128)(2,1)}), bf16[8,672,128]{2,1,0:T(8,128)(2,1)S(1)}, u32[]{:S(2)}, u32[]{:S(2)}) %all-to-all-start) | async-done | bytes 1376288 | tf_op jit(solution)/shard_map/all_to_all | solution.py:51
  29.3 0.1 convert_reduce_fusion
  29.4 0.2 fusion.25
  29.7 1.9 %collective-permute-start = (f32[32,7,128]{2,0,1:T(8,128)S(1)}, f32[32,7,128]{2,0,1:T(8,128)S(1)}, u32[]{:S(2)}, u32[]{:S(2)}) collective-permute-start(f32[32,7,128]{2,0,1:T(8,128)S(1)} %bitcast.104), channel_id=1, source_target_pairs={{0,8},{8,0},{1,9},{9,1},{2,10},{10,2},{3,11},{11,3},{4,12},{12,4},... | collective-permute-start | bytes 344072 | tf_op jit(solution)/shard_map/ppermute | solution.py:69
  31.7 1.2 %collective-permute-done = f32[32,7,128]{2,0,1:T(8,128)S(1)} collective-permute-done((f32[32,7,128]{2,0,1:T(8,128)S(1)}, f32[32,7,128]{2,0,1:T(8,128)S(1)}, u32[]{:S(2)}, u32[]{:S(2)}) %collective-permute-start) | collective-permute-done | bytes 114720 | tf_op jit(solution)/shard_map/ppermute | solution.py:69
  33.0 0.7 pad.4.clone
  33.7 15.1 %all-to-all-start.1 = ((f32[32,8,128]{2,1,0:T(8,128)}), f32[32,8,128]{2,1,0:T(8,128)S(1)}, u32[]{:S(2)}, u32[]{:S(2)}) async-start(f32[32,8,128]{2,1,0:T(8,128)} %pad.4.clone), calls=%async_computation.1 | async-start | bytes 262144 | tf_op jit(solution)/shard_map/all_to_all | solution.py:71
  48.8 0.2 select_convert_fusion
  49.0 0.9 %broadcast_select_fusion.1 = bf16[8,224,128]{2,1,0:T(8,128)(2,1)} fusion(pred[8]{0:T(512)(128)(4,1)S(1)} %iota_compare_fusion.2, bf16[224,128]{1,0:T(8,128)(2,1)S(1)} %select_convert_fusion), kind=kLoop, calls=%fused_computation.6 | loop fusion | flops 229376 | bytes 516104 | tf_op jit(solution)/shard_map/jit(_where)/select_n | solution.py:62
  49.9 11.4 %all-to-all-done.1 = f32[32,8,128]{2,1,0:T(8,128)S(1)} async-done(((f32[32,8,128]{2,1,0:T(8,128)}), f32[32,8,128]{2,1,0:T(8,128)S(1)}, u32[]{:S(2)}, u32[]{:S(2)}) %all-to-all-start.1) | async-done | bytes 131104 | tf_op jit(solution)/shard_map/all_to_all | solution.py:71
  61.3 4.3 %all-to-all-start.2 = ((bf16[8,224,128]{2,1,0:T(8,128)(2,1)}), bf16[8,224,128]{2,1,0:T(8,128)(2,1)S(1)}, u32[]{:S(2)}, u32[]{:S(2)}) async-start(bf16[8,224,128]{2,1,0:T(8,128)(2,1)} %broadcast_select_fusion.1), calls=%async_computation.2 | async-start | bytes 917504 | tf_op jit(solution)/shard_map/all_to_all | solution.py:63
  65.6 0.9 %fusion.12 = (f32[1,4,7168]{2,1,0:T(4,128)}, f32[1,4,7168]{2,1,0:T(4,128)}, f32[1,4,7168]{2,1,0:T(4,128)}) fusion(f32[56,4,128]{2,1,0:T(4,128)S(1)} %bitcast.94, f32[1,4,7168]{2,1,0:T(4,128)S(1)} %copy-done, f32[1,4,7168]{2,1,0:T(4,128)S(1)} %copy-done.1, f32[1,4,7168]{2,1,0:T(4,128)S(1)} %copy-done.2), kind=kLoop, calls=%fused_computation.29 | loop fusion | flops 430080 | bytes 802816 | tf_op jit(solution)/shard_map/broadcast_in_dim;reshape | solution.py:90
  66.6 0.6 multiply_subtract_fusion
  67.2 5.3 %all-to-all-done.2 = bf16[8,224,128]{2,1,0:T(8,128)(2,1)S(1)} async-done(((bf16[8,224,128]{2,1,0:T(8,128)(2,1)}), bf16[8,224,128]{2,1,0:T(8,128)(2,1)S(1)}, u32[]{:S(2)}, u32[]{:S(2)}) %all-to-all-start.2) | async-done | bytes 458784 | tf_op jit(solution)/shard_map/all_to_all | solution.py:63
  72.5 0.2 compare_reduce_fusion
  72.7 0.1 select_reduce_fusion
  72.8 0.1 broadcast_select_fusion
  73.0 0.3 convolution_convert_fusion
  73.3 0.8 %broadcast_in_dim_reshape.15 = bf16[1,1,4,28672]{3,2,1,0:T(4,128)(2,1)} reshape(bf16[4,4,56,128]{3,2,1,0:T(8,128)(2,1)S(1)} %copy.71) | data formatting | bytes 458752 | tf_op jit(solution)/shard_map/broadcast_in_dim;reshape | solution.py:94
  (28 shorter events, 0.5 us)
Async XLA Ops:
  3.0 1.1 %copy-start.3 = (bf16[1,1,32,7168]{3,2,1,0:T(8,128)(2,1)S(1)}, bf16[1,1,32,7168]{3,2,1,0:T(8,128)(2,1)}, u32[]{:S(2)}) copy-start(bf16[1,1,32,7168]{3,2,1,0:T(8,128)(2,1)} %param.10) | copy-start | bytes 1376260
  5.6 9.4 %copy-start.1 = (f32[1,4,7168]{2,1,0:T(4,128)S(1)}, f32[1,4,7168]{2,1,0:T(4,128)}, u32[]{:S(2)}) copy-start(f32[1,4,7168]{2,1,0:T(4,128)} %param.12) | copy-start | bytes 344068
  5.6 10.8 %copy-start = (f32[1,4,7168]{2,1,0:T(4,128)S(1)}, f32[1,4,7168]{2,1,0:T(4,128)}, u32[]{:S(2)}) copy-start(f32[1,4,7168]{2,1,0:T(4,128)} %param.13) | copy-start | bytes 344068
  5.6 23.6 %all-to-all-start = ((bf16[8,672,128]{2,1,0:T(8,128)(2,1)}), bf16[8,672,128]{2,1,0:T(8,128)(2,1)S(1)}, u32[]{:S(2)}, u32[]{:S(2)}) async-start(bf16[8,672,128]{2,1,0:T(8,128)(2,1)} %pad_maximum_fusion), calls=%async_computation | async-start | bytes 2752512 | tf_op jit(solution)/shard_map/all_to_all | solution.py:51
  29.4 19.3 %copy-start.2 = (f32[1,4,7168]{2,1,0:T(4,128)S(1)}, f32[1,4,7168]{2,1,0:T(4,128)}, u32[]{:S(2)}) copy-start(f32[1,4,7168]{2,1,0:T(4,128)} %param.11) | copy-start | bytes 344068
  29.7 3.2 %collective-permute-start = (f32[32,7,128]{2,0,1:T(8,128)S(1)}, f32[32,7,128]{2,0,1:T(8,128)S(1)}, u32[]{:S(2)}, u32[]{:S(2)}) collective-permute-start(f32[32,7,128]{2,0,1:T(8,128)S(1)} %bitcast.104), channel_id=1, source_target_pairs={{0,8},{8,0},{1,9},{9,1},{2,10},{10,2},{3,11},{11,3},{4,12},{12,4},... | collective-permute-start | bytes 344072 | tf_op jit(solution)/shard_map/ppermute | solution.py:69
  33.7 27.7 %all-to-all-start.1 = ((f32[32,8,128]{2,1,0:T(8,128)}), f32[32,8,128]{2,1,0:T(8,128)S(1)}, u32[]{:S(2)}, u32[]{:S(2)}) async-start(f32[32,8,128]{2,1,0:T(8,128)} %pad.4.clone), calls=%async_computation.1 | async-start | bytes 262144 | tf_op jit(solution)/shard_map/all_to_all | solution.py:71
  48.7 17.8 %copy-start.4 = (f32[896]{0:T(1024)S(1)}, f32[896]{0:T(1024)}, u32[]{:S(2)}) copy-start(f32[896]{0:T(1024)} %param.15) | copy-start | bytes 10756
  48.8 17.8 %copy-start.5 = (f32[896]{0:T(1024)S(1)}, f32[896]{0:T(1024)}, u32[]{:S(2)}) copy-start(f32[896]{0:T(1024)} %param.16) | copy-start | bytes 10756
  48.8 17.8 %copy-start.6 = (f32[896]{0:T(1024)S(1)}, f32[896]{0:T(1024)}, u32[]{:S(2)}) copy-start(f32[896]{0:T(1024)} %param.17) | copy-start | bytes 10756
  61.3 11.1 %all-to-all-start.2 = ((bf16[8,224,128]{2,1,0:T(8,128)(2,1)}), bf16[8,224,128]{2,1,0:T(8,128)(2,1)S(1)}, u32[]{:S(2)}, u32[]{:S(2)}) async-start(bf16[8,224,128]{2,1,0:T(8,128)(2,1)} %broadcast_select_fusion.1), calls=%async_computation.2 | async-start | bytes 917504 | tf_op jit(solution)/shard_map/all_to_all | solution.py:63

commit v2 on v1

--- a/solution.py
+++ b/solution.py
@@ -2,6 +2,7 @@
 import jax.numpy as jnp
 from jax import lax
 from jax.sharding import Mesh, PartitionSpec as P
+
 
 BETA_FIRST = 0.9
 BETA_SECOND = 0.95
@@ -43,14 +44,21 @@
     writer,
     live_blocks,
 ):
-    expert_part = expert_grads[0, 0].reshape(8, 4, 56, 128).transpose(0, 2, 1, 3)
-    expert_part = expert_part.reshape(8, 224, 128)
-    dense_part = dense_grads[0, 0].reshape(8, 8, 8, 7, 128).transpose(2, 0, 3, 1, 4)
-    dense_part = dense_part.reshape(8, 448, 128)
-    outgoing = jnp.concatenate([expert_part, dense_part], axis=1)
+    outgoing = expert_grads[0, 0].reshape(8, 4, 7168)
     arrived = lax.all_to_all(outgoing, EDP, split_axis=0, concat_axis=0, tiled=True)
-    expert_sum = arrived[:, :224].astype(jnp.float32).sum(axis=0)
-    dense_partial = arrived[:, 224:].astype(jnp.float32).sum(axis=0)
+    expert_sum = to_tiles(arrived.astype(jnp.float32).sum(axis=0))
+
+    core = lax.axis_index("c")
+    out_row = lax.broadcasted_iota(jnp.int32, (64, 64), 0)
+    in_row = lax.broadcasted_iota(jnp.int32, (64, 64), 1)
+    wanted = 2 * (out_row % 32) + jnp.where(out_row < 32, core, 1 - core)
+    parting = (in_row == wanted).astype(jnp.bfloat16)
+    parted = jnp.dot(parting, dense_grads[0, 0], preferred_element_type=jnp.float32)
+    parted = parted.astype(jnp.bfloat16)
+    swapped = lax.ppermute(parted[32:], "c", [(0, 1), (1, 0)])
+    pair = parted[:32].astype(jnp.float32) + swapped.astype(jnp.float32)
+    pair = pair.astype(jnp.bfloat16).reshape(4, 8, 8, 7, 128).transpose(2, 0, 3, 1, 4)
+    pair = pair.reshape(8, 224, 128)
 
     expert_new, expert_mom, expert_sec = adam_update(
         to_tiles(expert_param[0]), to_tiles(expert_moment[0]), to_tiles(expert_second[0]), expert_sum
@@ -60,15 +68,15 @@
     kept = jnp.where(block < live_blocks[0, 0], expert_new, 0.0).astype(jnp.bfloat16)
     rank = lax.broadcasted_iota(jnp.int32, (8, 224, 128), 0)
     slices = jnp.where(rank == writer[0, 0, 0], kept[None], jnp.bfloat16(ABSENT))
-    received = lax.all_to_all(slices, EDP, split_axis=0, concat_axis=0, tiled=True)
 
-    core = lax.axis_index("c")
-    rows = dense_partial.reshape(8, 7, 8, 128).transpose(0, 2, 1, 3).reshape(32, 2, 7, 128)
-    mine = jnp.where(core == 0, rows[:, 0], rows[:, 1])
-    other = jnp.where(core == 0, rows[:, 1], rows[:, 0])
-    swapped = lax.ppermute(other, "c", [(0, 1), (1, 0)])
-    pair = jnp.pad(mine + swapped, ((0, 0), (0, 1), (0, 0)))
-    dense_arrived = lax.all_to_all(pair, ("z", "yh"), split_axis=0, concat_axis=0, tiled=True)
+    second = jnp.concatenate([slices, pair], axis=1)
+    both = lax.all_to_all(second, EDP, split_axis=0, concat_axis=0, tiled=True)
+    received = both[:, :224]
+    partial = both[:, 224:].astype(jnp.float32).sum(axis=0)
+
+    rows = partial.reshape(4, 7, 8, 128).transpose(0, 2, 1, 3).reshape(32, 7, 128)
+    rows = jnp.pad(rows, ((0, 0), (0, 1), (0, 0)))
+    dense_arrived = lax.all_to_all(rows, ("z", "yh"), split_axis=0, concat_axis=0, tiled=True)
     dense_sum = dense_arrived.sum(axis=0)[:7].reshape(-1)
 
     present = (received[:, 0, 0].astype(jnp.float32) < ABSENT / 2)

time: 74.5 us -> 67.9 us (0.911)
  blocking collectives: 0 us -> 17.1 us
  waiting for transfers between devices: 30.7 us -> 18.3 us
  starting transfers between devices: 30.7 us -> 22.6 us
  other arithmetic: 4.85 us -> 2.82 us
  local copies, waits for them, and re-layouts: 5.36 us -> 3.76 us
    all_to_all x0 -> x1, blocking collectives: none -> 17.1 us  [body(): both = lax.all_to_all(second, EDP, split_axis=0, concat_axis=0, tiled=True)]
    all_to_all x2 -> x1, starting transfers between devices: 19.3 us -> 11.4 us  [body(): lax.all_to_all(rows, ('z', 'yh'), split_axis=0, concat_axis=0, tiled=True)]
    all_to_all x2 -> x1, waiting for transfers between devices: 16.7 us -> 11 us  [body(): lax.all_to_all(rows, ('z', 'yh'), split_axis=0, concat_axis=0, tiled=True)]
    all_to_all x1, waiting for transfers between devices: 12.8 us -> 7.33 us  [body(): lax.all_to_all(outgoing, EDP, split_axis=0, concat_axis=0, tiled=True)]
    another operation x1, local copies, waits for them, and re-layouts: 2.36 us -> 0.94 us  [body(): outgoing = expert_grads[0, 0].reshape(8, 4, 7168)]
    ppermute x1, waiting for transfers between devices: 1.22 us -> 0.01 us  [body(): swapped = lax.ppermute(parted[32:], 'c', [(0, 1), (1, 0)])]
    transpose x3 -> x2, local copies, waits for them, and re-layouts: 1.27 us -> 0.05 us  [the longest x1 0.04 us: body(): pair.astype(jnp.bfloat16).reshape(4, 8, 8, 7, 128).transpose(2, 0, 3, 1, 4)]
    concatenate x1, other arithmetic: 1.19 us -> 0.06 us  [body(): second = jnp.concatenate([slices, pair], axis=1)]
  transfers between devices with their start and end apart: 4 -> 3, of which waited for: 4 -> 2; matrix products, arithmetic and copies ran while one was open for 4% -> 4% of each run, Pallas kernels for 0% -> 0%
where the time goes in v2:
time: 67.9 us; the launch traced here: 67.6 us
  starting transfers between devices  22.6 us (33%)
  waiting for transfers between devices  18.3 us (27%)
  blocking collectives  17.1 us (25%)
  local copies, waits for them, and re-layouts  3.76 us (6%)
  other arithmetic  2.82 us (4%)
  between operations  2.22 us (3%)
  matrix products  0.72 us (1%)
    all_to_all x1, blocking collectives, body(): both = lax.all_to_all(second, EDP, split_axis=0, concat_axis=0, tiled=True)  17.1 us
    all_to_all x1, starting transfers between devices, body(): lax.all_to_all(rows, ('z', 'yh'), split_axis=0, concat_axis=0, tiled=True)  11.4 us
    all_to_all x1, waiting for transfers between devices, body(): lax.all_to_all(rows, ('z', 'yh'), split_axis=0, concat_axis=0, tiled=True)  11 us
    all_to_all x1, starting transfers between devices, body(): lax.all_to_all(outgoing, EDP, split_axis=0, concat_axis=0, tiled=True)  9.19 us
    all_to_all x1, waiting for transfers between devices, body(): lax.all_to_all(outgoing, EDP, split_axis=0, concat_axis=0, tiled=True)  7.33 us
    ppermute x1, starting transfers between devices, body(): swapped = lax.ppermute(parted[32:], 'c', [(0, 1), (1, 0)])  2.05 us
    sub x2, other arithmetic, adam_update(): master_new = master - LEARN_RATE * (direction + DECAY_RATE * master)  1.52 us
  transfers between devices with their start and end apart: 3, of which 2 were waited for; matrix products, arithmetic and copies ran while one was open for 4% of the time, Pallas kernels for 0%

profile of v2, /device:TPU:8, one launch (start us, length us, event | category | flops | bytes accessed | tf_op | source)
XLA Modules:
  0.0 67.6 jit_solution(12327544009199988066)
XLA Ops:
  0.7 1.1 %copy-done = bf16[1,1,64,7168]{3,2,1,0:T(8,128)(2,1)S(1)} copy-done((bf16[1,1,64,7168]{3,2,1,0:T(8,128)(2,1)S(1)}, bf16[1,1,64,7168]{3,2,1,0:T(8,128)(2,1)}, u32[]{:S(2)}) %copy-start) | copy-done | bytes 917528
  1.8 0.4 convolution_convert_fusion
  2.3 2.1 %collective-permute-start = (bf16[32,7168]{1,0:T(8,128)(2,1)S(1)}, bf16[32,7168]{1,0:T(8,128)(2,1)S(1)}, u32[]{:S(2)}, u32[]{:S(2)}) collective-permute-start(bf16[32,7168]{1,0:T(8,128)(2,1)S(1)} %slice.26), channel_id=1, source_target_pairs={{0,8},{8,0},{1,9},{9,1},{2,10},{10,2},{3,11},{11,3},{4,12},{12,4},... | collective-permute-start | bytes 1376264 | tf_op jit(solution)/shard_map/ppermute | solution.py:58
  4.4 0.9 %reshape_squeeze.8 = bf16[8,4,7168]{2,1,0:T(4,128)(2,1)} reshape(bf16[1,1,32,7168]{3,2,1,0:T(8,128)(2,1)S(1)} %copy-done.1) | data formatting | bytes 917504 | tf_op jit(solution)/shard_map/reshape;squeeze | solution.py:47
  5.3 9.2 %all-to-all-start = ((bf16[8,4,7168]{2,1,0:T(4,128)(2,1)}), bf16[8,4,7168]{2,1,0:T(4,128)(2,1)S(1)}, u32[]{:S(2)}, u32[]{:S(2)}) async-start(bf16[8,4,7168]{2,1,0:T(4,128)(2,1)} %reshape_squeeze.8), calls=%async_computation | async-start | bytes 917504 | tf_op jit(solution)/shard_map/all_to_all | solution.py:48
  15.9 0.1 add_convert_fusion
  16.1 7.3 %all-to-all-done = bf16[8,4,7168]{2,1,0:T(4,128)(2,1)S(1)} async-done(((bf16[8,4,7168]{2,1,0:T(4,128)(2,1)}), bf16[8,4,7168]{2,1,0:T(4,128)(2,1)S(1)}, u32[]{:S(2)}, u32[]{:S(2)}) %all-to-all-start) | async-done | bytes 458784 | tf_op jit(solution)/shard_map/all_to_all | solution.py:48
  23.4 0.2 convert_reduce_fusion.1
  23.6 0.9 %multiply_subtract_fusion = (f32[1,4,7168]{2,1,0:T(4,128)}, f32[1,4,7168]{2,1,0:T(4,128)}, f32[1,4,7168]{2,1,0:T(4,128)}, f32[1,4,7168]{2,1,0:T(4,128)S(1)}, f32[1,4,7168]{2,1,0:T(4,128)S(1)}) fusion(f32[1,4,7168]{2,1,0:T(4,128)S(1)} %copy-done.2, f32[4,7168]{1,0:T(4,128)S(1)} %convert_reduce_fusion.1, f32[1,4,7168]{2,1,0:T(4,128)S(1)} %copy-done.3, ...), kind=kLoop, calls=%fused_computation.24 | loop fusion | flops 430080 | bytes 1032192 | tf_op jit(solution)/shard_map/sub | solution.py:23
  24.5 0.2 select_convert_fusion
  24.8 0.1 broadcast_select_fusion
  24.9 0.1 pad_maximum_fusion
  24.9 17.1 %all_to_all.15 = bf16[8,448,128]{2,1,0:T(8,128)(2,1)S(1)} all-to-all(bf16[8,448,128]{2,1,0:T(8,128)(2,1)S(1)} %pad_maximum_fusion), channel_id=1, replica_groups=mesh['z'=8,'yh'=4,'c'=2,'yl'=2,'x'=4] {'yl','x'}, dimensions={0} | all-to-all | bytes 1835008 | tf_op jit(solution)/shard_map/all_to_all | solution.py:73
  42.1 0.1 convert_reduce_fusion
  42.2 0.1 copy.62
  42.3 0.7 pad.4.clone
  42.9 11.4 %all-to-all-start.2 = ((f32[32,8,128]{2,1,0:T(8,128)}), f32[32,8,128]{2,1,0:T(8,128)S(1)}, u32[]{:S(2)}, u32[]{:S(2)}) async-start(f32[32,8,128]{2,1,0:T(8,128)} %pad.4.clone), calls=%async_computation.2 | async-start | bytes 262144 | tf_op jit(solution)/shard_map/all_to_all | solution.py:79
  54.3 0.2 compare_reduce_fusion
  54.5 0.1 slice_select_fusion
  54.7 0.1 select_reduce_fusion
  54.8 0.3 convolution_convert_fusion.1
  55.1 0.8 %broadcast_in_dim_reshape.2 = bf16[1,1,4,28672]{3,2,1,0:T(4,128)(2,1)} reshape(bf16[4,4,56,128]{3,2,1,0:T(8,128)(2,1)S(1)} %copy.61) | data formatting | bytes 458752 | tf_op jit(solution)/shard_map/broadcast_in_dim;reshape | solution.py:102
  55.9 11.0 %all-to-all-done.2 = f32[32,8,128]{2,1,0:T(8,128)S(1)} async-done(((f32[32,8,128]{2,1,0:T(8,128)}), f32[32,8,128]{2,1,0:T(8,128)S(1)}, u32[]{:S(2)}, u32[]{:S(2)}) %all-to-all-start.2) | async-done | bytes 131104 | tf_op jit(solution)/shard_map/all_to_all | solution.py:79
  66.9 0.6 multiply_subtract_fusion.1
  (28 shorter events, 0.3 us)
Async XLA Ops:
  0.6 1.2 %copy-start = (bf16[1,1,64,7168]{3,2,1,0:T(8,128)(2,1)S(1)}, bf16[1,1,64,7168]{3,2,1,0:T(8,128)(2,1)}, u32[]{:S(2)}) copy-start(bf16[1,1,64,7168]{3,2,1,0:T(8,128)(2,1)} %param.14) | copy-start | bytes 2752516
  2.3 2.1 %copy-start.1 = (bf16[1,1,32,7168]{3,2,1,0:T(8,128)(2,1)S(1)}, bf16[1,1,32,7168]{3,2,1,0:T(8,128)(2,1)}, u32[]{:S(2)}) copy-start(bf16[1,1,32,7168]{3,2,1,0:T(8,128)(2,1)} %param.10) | copy-start | bytes 1376260
  2.3 13.5 %collective-permute-start = (bf16[32,7168]{1,0:T(8,128)(2,1)S(1)}, bf16[32,7168]{1,0:T(8,128)(2,1)S(1)}, u32[]{:S(2)}, u32[]{:S(2)}) collective-permute-start(bf16[32,7168]{1,0:T(8,128)(2,1)S(1)} %slice.26), channel_id=1, source_target_pairs={{0,8},{8,0},{1,9},{9,1},{2,10},{10,2},{3,11},{11,3},{4,12},{12,4},... | collective-permute-start | bytes 1376264 | tf_op jit(solution)/shard_map/ppermute | solution.py:58
  5.3 18.1 %all-to-all-start = ((bf16[8,4,7168]{2,1,0:T(4,128)(2,1)}), bf16[8,4,7168]{2,1,0:T(4,128)(2,1)S(1)}, u32[]{:S(2)}, u32[]{:S(2)}) async-start(bf16[8,4,7168]{2,1,0:T(4,128)(2,1)} %reshape_squeeze.8), calls=%async_computation | async-start | bytes 917504 | tf_op jit(solution)/shard_map/all_to_all | solution.py:48
  16.0 7.6 %copy-start.2 = (f32[1,4,7168]{2,1,0:T(4,128)S(1)}, f32[1,4,7168]{2,1,0:T(4,128)}, u32[]{:S(2)}) copy-start(f32[1,4,7168]{2,1,0:T(4,128)} %param.11) | copy-start | bytes 344068
  16.0 7.6 %copy-start.3 = (f32[1,4,7168]{2,1,0:T(4,128)S(1)}, f32[1,4,7168]{2,1,0:T(4,128)}, u32[]{:S(2)}) copy-start(f32[1,4,7168]{2,1,0:T(4,128)} %param.12) | copy-start | bytes 344068
  16.0 7.6 %copy-start.4 = (f32[1,4,7168]{2,1,0:T(4,128)S(1)}, f32[1,4,7168]{2,1,0:T(4,128)}, u32[]{:S(2)}) copy-start(f32[1,4,7168]{2,1,0:T(4,128)} %param.13) | copy-start | bytes 344068
  42.9 24.0 %all-to-all-start.2 = ((f32[32,8,128]{2,1,0:T(8,128)}), f32[32,8,128]{2,1,0:T(8,128)S(1)}, u32[]{:S(2)}, u32[]{:S(2)}) async-start(f32[32,8,128]{2,1,0:T(8,128)} %pad.4.clone), calls=%async_computation.2 | async-start | bytes 262144 | tf_op jit(solution)/shard_map/all_to_all | solution.py:79
  54.6 12.3 %copy-start.5 = (f32[896]{0:T(1024)S(1)}, f32[896]{0:T(1024)}, u32[]{:S(2)}) copy-start(f32[896]{0:T(1024)} %param.15) | copy-start | bytes 10756
  54.7 12.3 %copy-start.6 = (f32[896]{0:T(1024)S(1)}, f32[896]{0:T(1024)}, u32[]{:S(2)}) copy-start(f32[896]{0:T(1024)} %param.16) | copy-start | bytes 10756
  54.7 12.3 %copy-start.7 = (f32[896]{0:T(1024)S(1)}, f32[896]{0:T(1024)}, u32[]{:S(2)}) copy-start(f32[896]{0:T(1024)} %param.17) | copy-start | bytes 10756

commit v3 on v2

--- a/solution.py
+++ b/solution.py
@@ -47,6 +47,7 @@
     outgoing = expert_grads[0, 0].reshape(8, 4, 7168)
     arrived = lax.all_to_all(outgoing, EDP, split_axis=0, concat_axis=0, tiled=True)
     expert_sum = to_tiles(arrived.astype(jnp.float32).sum(axis=0))
+    state = (to_tiles(expert_param[0]), to_tiles(expert_moment[0]), to_tiles(expert_second[0]))
 
     core = lax.axis_index("c")
     out_row = lax.broadcasted_iota(jnp.int32, (64, 64), 0)
@@ -60,9 +61,7 @@
     pair = pair.astype(jnp.bfloat16).reshape(4, 8, 8, 7, 128).transpose(2, 0, 3, 1, 4)
     pair = pair.reshape(8, 224, 128)
 
-    expert_new, expert_mom, expert_sec = adam_update(
-        to_tiles(expert_param[0]), to_tiles(expert_moment[0]), to_tiles(expert_second[0]), expert_sum
-    )
+    expert_new, _, _ = adam_update(*state, expert_sum)
     row = lax.broadcasted_iota(jnp.int32, (224, 128), 0)
     block = (row % 4) * 56 + row // 4
     kept = jnp.where(block < live_blocks[0, 0], expert_new, 0.0).astype(jnp.bfloat16)
@@ -71,13 +70,21 @@
 
     second = jnp.concatenate([slices, pair], axis=1)
     both = lax.all_to_all(second, EDP, split_axis=0, concat_axis=0, tiled=True)
-    received = both[:, :224]
     partial = both[:, 224:].astype(jnp.float32).sum(axis=0)
 
     rows = partial.reshape(4, 7, 8, 128).transpose(0, 2, 1, 3).reshape(32, 7, 128)
-    rows = jnp.pad(rows, ((0, 0), (0, 1), (0, 0)))
-    dense_arrived = lax.all_to_all(rows, ("z", "yh"), split_axis=0, concat_axis=0, tiled=True)
-    dense_sum = dense_arrived.sum(axis=0)[:7].reshape(-1)
+    rows = rows.astype(jnp.bfloat16)
+    last = lax.all_to_all(rows, ("z", "yh"), split_axis=0, concat_axis=0, tiled=True)
+    dense_sum = last.astype(jnp.float32).sum(axis=0).reshape(-1)
+
+    state, expert_sum, both, _ = lax.optimization_barrier((state, expert_sum, both, rows))
+    received = both[:, :224]
+    expert_new, expert_mom, expert_sec = adam_update(*state, expert_sum)
+    expert_new, expert_mom, expert_sec = (
+        from_tiles(expert_new),
+        from_tiles(expert_mom),
+        from_tiles(expert_sec),
+    )
 
     present = (received[:, 0, 0].astype(jnp.float32) < ABSENT / 2)
     index = lax.broadcasted_iota(jnp.int32, (8, 8), 0)
@@ -87,15 +94,16 @@
     selector = ((slot == before[None, :]) & present[None, :]).astype(jnp.bfloat16)
     clean = jnp.where(present[:, None, None], received, jnp.bfloat16(0))
     saved = jnp.einsum("kr,rql->kql", selector, clean, preferred_element_type=jnp.float32)
-    saved = saved.astype(jnp.bfloat16).reshape(4, 56, 4, 128).transpose(0, 2, 1, 3).reshape(4, 28672)
+    saved = saved.astype(jnp.bfloat16).reshape(4, 56, 4, 128)
+    saved = saved.transpose(0, 2, 1, 3).reshape(4, 28672)
 
     dense_new, dense_mom, dense_sec = adam_update(
         dense_param, dense_moment, dense_second, dense_sum
     )
     return (
-        from_tiles(expert_new)[None],
-        from_tiles(expert_mom)[None],
-        from_tiles(expert_sec)[None],
+        expert_new[None],
+        expert_mom[None],
+        expert_sec[None],
         dense_new,
         dense_mom,
         dense_sec,

time: 67.9 us -> 67.2 us (0.990)
  the two profiles are of different devices: /device:TPU:8 before, /device:TPU:1 now
where the time goes in v3:
time: 67.2 us; the launch traced here: 65.9 us
  starting transfers between devices  23.4 us (35%)
  blocking collectives  17.2 us (26%)
  waiting for transfers between devices  16 us (24%)
  local copies, waits for them, and re-layouts  3.67 us (5%)
  other arithmetic  2.7 us (4%)
  between operations  2.2 us (3%)
  matrix products  0.72 us (1%)
    all_to_all x1, blocking collectives, body(): both = lax.all_to_all(second, EDP, split_axis=0, concat_axis=0, tiled=True)  17.2 us
    all_to_all x1, starting transfers between devices, body(): lax.all_to_all(rows, ('z', 'yh'), split_axis=0, concat_axis=0, tiled=True)  11.1 us
    all_to_all x1, waiting for transfers between devices, body(): lax.all_to_all(rows, ('z', 'yh'), split_axis=0, concat_axis=0, tiled=True)  9.31 us
    ppermute x1, starting transfers between devices, body(): swapped = lax.ppermute(parted[32:], 'c', [(0, 1), (1, 0)])  8.88 us
    all_to_all x1, waiting for transfers between devices, body(): lax.all_to_all(outgoing, EDP, split_axis=0, concat_axis=0, tiled=True)  6.66 us
    all_to_all x1, starting transfers between devices, body(): lax.all_to_all(outgoing, EDP, split_axis=0, concat_axis=0, tiled=True)  3.47 us
    sub x2, other arithmetic, adam_update(): master_new = master - LEARN_RATE * (direction + DECAY_RATE * master)  1.39 us
  transfers between devices with their start and end apart: 3, of which 2 were waited for; matrix products, arithmetic and copies ran while one was open for 5% of the time, Pallas kernels for 0%

profile of v3, /device:TPU:1, one launch (start us, length us, event | category | flops | bytes accessed | tf_op | source)
XLA Modules:
  0.0 65.9 jit_solution(11072909900830588721)
XLA Ops:
  0.7 1.1 %copy-done = bf16[1,1,64,7168]{3,2,1,0:T(8,128)(2,1)S(1)} copy-done((bf16[1,1,64,7168]{3,2,1,0:T(8,128)(2,1)S(1)}, bf16[1,1,64,7168]{3,2,1,0:T(8,128)(2,1)}, u32[]{:S(2)}) %copy-start) | copy-done | bytes 917528
  1.8 0.4 convolution_convert_fusion
  2.3 8.9 %collective-permute-start = (bf16[32,7168]{1,0:T(8,128)(2,1)S(1)}, bf16[32,7168]{1,0:T(8,128)(2,1)S(1)}, u32[]{:S(2)}, u32[]{:S(2)}) collective-permute-start(bf16[32,7168]{1,0:T(8,128)(2,1)S(1)} %slice.22), channel_id=1, source_target_pairs={{0,8},{8,0},{1,9},{9,1},{2,10},{10,2},{3,11},{11,3},{4,12},{12,4},... | collective-permute-start | bytes 1376264 | tf_op jit(solution)/shard_map/ppermute | solution.py:59
  11.2 0.9 %reshape_squeeze.15 = bf16[8,4,7168]{2,1,0:T(4,128)(2,1)} reshape(bf16[1,1,32,7168]{3,2,1,0:T(8,128)(2,1)S(1)} %copy-done.4) | data formatting | bytes 917504 | tf_op jit(solution)/shard_map/reshape;squeeze | solution.py:47
  12.2 3.5 %all-to-all-start = ((bf16[8,4,7168]{2,1,0:T(4,128)(2,1)}), bf16[8,4,7168]{2,1,0:T(4,128)(2,1)S(1)}, u32[]{:S(2)}, u32[]{:S(2)}) async-start(bf16[8,4,7168]{2,1,0:T(4,128)(2,1)} %reshape_squeeze.15), calls=%async_computation | async-start | bytes 917504 | tf_op jit(solution)/shard_map/all_to_all | solution.py:48
  17.0 0.1 add_convert_fusion
  17.2 6.7 %all-to-all-done = bf16[8,4,7168]{2,1,0:T(4,128)(2,1)S(1)} async-done(((bf16[8,4,7168]{2,1,0:T(4,128)(2,1)}), bf16[8,4,7168]{2,1,0:T(4,128)(2,1)S(1)}, u32[]{:S(2)}, u32[]{:S(2)}) %all-to-all-start) | async-done | bytes 458784 | tf_op jit(solution)/shard_map/all_to_all | solution.py:48
  23.8 0.2 convert_reduce_fusion
  24.1 0.3 select_convert_fusion
  24.3 0.1 broadcast_select_fusion
  24.4 0.1 pad_maximum_fusion
  24.5 17.2 %all_to_all.15 = bf16[8,448,128]{2,1,0:T(8,128)(2,1)S(1)} all-to-all(bf16[8,448,128]{2,1,0:T(8,128)(2,1)S(1)} %pad_maximum_fusion), channel_id=1, replica_groups=mesh['z'=8,'yh'=4,'c'=2,'yl'=2,'x'=4] {'yl','x'}, dimensions={0} | all-to-all | bytes 1835008 | tf_op jit(solution)/shard_map/all_to_all | solution.py:72
  41.7 0.1 slice_reduce_fusion
  41.8 0.2 compare_reduce_fusion
  42.0 0.1 slice_select_fusion
  42.1 0.1 select_reduce_fusion
  42.2 0.6 copy.54
  42.9 11.1 %all-to-all-start.2 = ((bf16[32,7,128]{2,1,0:T(8,128)(2,1)}), bf16[32,7,128]{2,1,0:T(8,128)(2,1)S(1)}, u32[]{:S(2)}, u32[]{:S(2)}) async-start(bf16[32,7,128]{2,1,0:T(8,128)(2,1)} %copy.54), calls=%async_computation.2 | async-start | bytes 131072 | tf_op jit(solution)/shard_map/all_to_all | solution.py:77
  54.0 0.8 %multiply_subtract_fusion = (f32[224,128]{1,0:T(8,128)}, f32[224,128]{1,0:T(8,128)}, f32[224,128]{1,0:T(8,128)}) fusion(f32[224,128]{1,0:T(8,128)S(1)} %bitcast.75, f32[224,128]{1,0:T(8,128)S(1)} %bitcast.72, f32[224,128]{1,0:T(8,128)S(1)} %bitcast.77, f32[224,128]{1,0:T(8,128)S(1)} %bitcast.79), kind=kLoop, calls=%fused_computation.20 | loop fusion | flops 430080 | bytes 802816 | tf_op jit(solution)/shard_map/sub | solution.py:23
  54.8 0.3 convolution_convert_fusion.1
  55.0 0.1 copy.56
  55.1 0.8 %broadcast_in_dim_reshape.15 = bf16[1,1,4,28672]{3,2,1,0:T(4,128)(2,1)} reshape(bf16[4,4,56,128]{3,2,1,0:T(8,128)(2,1)S(1)} %copy.56) | data formatting | bytes 458752 | tf_op jit(solution)/shard_map/broadcast_in_dim;reshape | solution.py:110
  55.9 9.3 %all-to-all-done.2 = bf16[32,7,128]{2,1,0:T(8,128)(2,1)S(1)} async-done(((bf16[32,7,128]{2,1,0:T(8,128)(2,1)}), bf16[32,7,128]{2,1,0:T(8,128)(2,1)S(1)}, u32[]{:S(2)}, u32[]{:S(2)}) %all-to-all-start.2) | async-done | bytes 57376 | tf_op jit(solution)/shard_map/all_to_all | solution.py:77
  65.2 0.6 multiply_subtract_fusion.1
  (27 shorter events, 0.2 us)
Async XLA Ops:
  0.6 1.2 %copy-start = (bf16[1,1,64,7168]{3,2,1,0:T(8,128)(2,1)S(1)}, bf16[1,1,64,7168]{3,2,1,0:T(8,128)(2,1)}, u32[]{:S(2)}) copy-start(bf16[1,1,64,7168]{3,2,1,0:T(8,128)(2,1)} %param.14) | copy-start | bytes 2752516
  2.3 8.9 %copy-start.4 = (bf16[1,1,32,7168]{3,2,1,0:T(8,128)(2,1)S(1)}, bf16[1,1,32,7168]{3,2,1,0:T(8,128)(2,1)}, u32[]{:S(2)}) copy-start(bf16[1,1,32,7168]{3,2,1,0:T(8,128)(2,1)} %param.10) | copy-start | bytes 1376260
  2.3 14.7 %collective-permute-start = (bf16[32,7168]{1,0:T(8,128)(2,1)S(1)}, bf16[32,7168]{1,0:T(8,128)(2,1)S(1)}, u32[]{:S(2)}, u32[]{:S(2)}) collective-permute-start(bf16[32,7168]{1,0:T(8,128)(2,1)S(1)} %slice.22), channel_id=1, source_target_pairs={{0,8},{8,0},{1,9},{9,1},{2,10},{10,2},{3,11},{11,3},{4,12},{12,4},... | collective-permute-start | bytes 1376264 | tf_op jit(solution)/shard_map/ppermute | solution.py:59
  12.2 11.7 %all-to-all-start = ((bf16[8,4,7168]{2,1,0:T(4,128)(2,1)}), bf16[8,4,7168]{2,1,0:T(4,128)(2,1)S(1)}, u32[]{:S(2)}, u32[]{:S(2)}) async-start(bf16[8,4,7168]{2,1,0:T(4,128)(2,1)} %reshape_squeeze.15), calls=%async_computation | async-start | bytes 917504 | tf_op jit(solution)/shard_map/all_to_all | solution.py:48
  17.1 6.9 %copy-start.1 = (f32[1,4,7168]{2,1,0:T(4,128)S(1)}, f32[1,4,7168]{2,1,0:T(4,128)}, u32[]{:S(2)}) copy-start(f32[1,4,7168]{2,1,0:T(4,128)} %param.11) | copy-start | bytes 344068
  17.1 6.9 %copy-start.2 = (f32[1,4,7168]{2,1,0:T(4,128)S(1)}, f32[1,4,7168]{2,1,0:T(4,128)}, u32[]{:S(2)}) copy-start(f32[1,4,7168]{2,1,0:T(4,128)} %param.12) | copy-start | bytes 344068
  17.1 6.9 %copy-start.3 = (f32[1,4,7168]{2,1,0:T(4,128)S(1)}, f32[1,4,7168]{2,1,0:T(4,128)}, u32[]{:S(2)}) copy-start(f32[1,4,7168]{2,1,0:T(4,128)} %param.13) | copy-start | bytes 344068
  42.9 22.3 %all-to-all-start.2 = ((bf16[32,7,128]{2,1,0:T(8,128)(2,1)}), bf16[32,7,128]{2,1,0:T(8,128)(2,1)S(1)}, u32[]{:S(2)}, u32[]{:S(2)}) async-start(bf16[32,7,128]{2,1,0:T(8,128)(2,1)} %copy.54), calls=%async_computation.2 | async-start | bytes 131072 | tf_op jit(solution)/shard_map/all_to_all | solution.py:77
  54.7 10.5 %copy-start.5 = (f32[896]{0:T(1024)S(1)}, f32[896]{0:T(1024)}, u32[]{:S(2)}) copy-start(f32[896]{0:T(1024)} %param.15) | copy-start | bytes 10756
  54.8 10.5 %copy-start.6 = (f32[896]{0:T(1024)S(1)}, f32[896]{0:T(1024)}, u32[]{:S(2)}) copy-start(f32[896]{0:T(1024)} %param.16) | copy-start | bytes 10756
  54.8 10.5 %copy-start.7 = (f32[896]{0:T(1024)S(1)}, f32[896]{0:T(1024)}, u32[]{:S(2)}) copy-start(f32[896]{0:T(1024)} %param.17) | copy-start | bytes 10756

commit v4 on v3

--- a/solution.py
+++ b/solution.py
@@ -11,8 +11,10 @@
 EPSILON = 1e-08
 FIRST_BIAS = 1.0 - BETA_FIRST**10
 SECOND_BIAS = 1.0 - BETA_SECOND**10
-EP = ("z", "yh", "c")
-EDP = ("yl", "x")
+EP = ("zy", "c")
+EDP = "r"
+FIRST = 30
+MEMBERS = [(FIRST + j) % 32 for j in range(32)]
 ABSENT = 2.0**100
 
 
@@ -74,7 +76,10 @@
 
     rows = partial.reshape(4, 7, 8, 128).transpose(0, 2, 1, 3).reshape(32, 7, 128)
     rows = rows.astype(jnp.bfloat16)
-    last = lax.all_to_all(rows, ("z", "yh"), split_axis=0, concat_axis=0, tiled=True)
+    rows = jnp.concatenate([rows[FIRST:], rows[:FIRST]], axis=0)
+    last = lax.all_to_all(
+        rows, "zy", split_axis=0, concat_axis=0, tiled=True, axis_index_groups=[MEMBERS]
+    )
     dense_sum = last.astype(jnp.float32).sum(axis=0).reshape(-1)
 
     state, expert_sum, both, _ = lax.optimization_barrier((state, expert_sum, both, rows))
@@ -112,9 +117,9 @@
 
 
 def solution(mesh):
-    fine = Mesh(mesh.devices.reshape(8, 4, 2, 2, 4), EP + EDP)
+    fine = Mesh(mesh.devices.reshape(32, 2, 8), EP + (EDP,))
     state = P(EP, EDP, None)
-    flat = P(EP + EDP)
+    flat = P(EP + (EDP,))
     return jax.shard_map(
         body,
         mesh=fine,

time: 67.2 us -> 62.9 us (0.936)
  the two profiles are of different devices: /device:TPU:1 before, /device:TPU:16 now
where the time goes in v4:
time: 62.9 us; the launch traced here: 62.5 us
  starting transfers between devices  22.3 us (35%)
  blocking collectives  17.7 us (28%)
  waiting for transfers between devices  13.3 us (21%)
  local copies, waits for them, and re-layouts  3.68 us (6%)
  other arithmetic  2.72 us (4%)
  between operations  2.21 us (4%)
  matrix products  0.72 us (1%)
    all_to_all x1, blocking collectives, body(): both = lax.all_to_all(second, EDP, split_axis=0, concat_axis=0, tiled=True)  17.7 us
    all_to_all x1, starting transfers between devices, body(): lax.all_to_all(rows, 'zy', split_axis=0, concat_axis=0, tiled=True, axis_...  14.9 us
    all_to_all x1, waiting for transfers between devices, body(): lax.all_to_all(outgoing, EDP, split_axis=0, concat_axis=0, tiled=True)  7.92 us
    all_to_all x1, waiting for transfers between devices, body(): lax.all_to_all(rows, 'zy', split_axis=0, concat_axis=0, tiled=True, axis_...  5.39 us
    all_to_all x1, starting transfers between devices, body(): lax.all_to_all(outgoing, EDP, split_axis=0, concat_axis=0, tiled=True)  5.32 us
    ppermute x1, starting transfers between devices, body(): swapped = lax.ppermute(parted[32:], 'c', [(0, 1), (1, 0)])  2.05 us
    sub x2, other arithmetic, adam_update(): master_new = master - LEARN_RATE * (direction + DECAY_RATE * master)  1.39 us
  transfers between devices with their start and end apart: 3, of which 2 were waited for; matrix products, arithmetic and copies ran while one was open for 5% of the time, Pallas kernels for 0%

profile of v4, /device:TPU:16, one launch (start us, length us, event | category | flops | bytes accessed | tf_op | source)
XLA Modules:
  0.0 62.5 jit_solution(6723833111413778975)
XLA Ops:
  0.7 1.1 %copy-done = bf16[1,1,64,7168]{3,2,1,0:T(8,128)(2,1)S(1)} copy-done((bf16[1,1,64,7168]{3,2,1,0:T(8,128)(2,1)S(1)}, bf16[1,1,64,7168]{3,2,1,0:T(8,128)(2,1)}, u32[]{:S(2)}) %copy-start) | copy-done | bytes 917528
  1.8 0.4 convolution_convert_fusion
  2.3 2.1 %collective-permute-start = (bf16[32,7168]{1,0:T(8,128)(2,1)S(1)}, bf16[32,7168]{1,0:T(8,128)(2,1)S(1)}, u32[]{:S(2)}, u32[]{:S(2)}) collective-permute-start(bf16[32,7168]{1,0:T(8,128)(2,1)S(1)} %slice.30), channel_id=1, source_target_pairs={{0,8},{8,0},{1,9},{9,1},{2,10},{10,2},{3,11},{11,3},{4,12},{12,4},... | collective-permute-start | bytes 1376264 | tf_op jit(solution)/shard_map/ppermute | solution.py:61
  4.4 0.9 %reshape_squeeze.15 = bf16[8,4,7168]{2,1,0:T(4,128)(2,1)} reshape(bf16[1,1,32,7168]{3,2,1,0:T(8,128)(2,1)S(1)} %copy-done.4) | data formatting | bytes 917504 | tf_op jit(solution)/shard_map/reshape;squeeze | solution.py:49
  5.3 5.3 %all-to-all-start = ((bf16[8,4,7168]{2,1,0:T(4,128)(2,1)}), bf16[8,4,7168]{2,1,0:T(4,128)(2,1)S(1)}, u32[]{:S(2)}, u32[]{:S(2)}) async-start(bf16[8,4,7168]{2,1,0:T(4,128)(2,1)} %reshape_squeeze.15), calls=%async_computation | async-start | bytes 917504 | tf_op jit(solution)/shard_map/all_to_all | solution.py:50
  12.0 0.1 add_convert_fusion
  12.2 7.9 %all-to-all-done = bf16[8,4,7168]{2,1,0:T(4,128)(2,1)S(1)} async-done(((bf16[8,4,7168]{2,1,0:T(4,128)(2,1)}), bf16[8,4,7168]{2,1,0:T(4,128)(2,1)S(1)}, u32[]{:S(2)}, u32[]{:S(2)}) %all-to-all-start) | async-done | bytes 458784 | tf_op jit(solution)/shard_map/all_to_all | solution.py:50
  20.1 0.2 convert_reduce_fusion
  20.3 0.3 select_convert_fusion
  20.6 0.1 broadcast_select_fusion
  20.7 0.1 pad_maximum_fusion
  20.8 17.7 %all_to_all.15 = bf16[8,448,128]{2,1,0:T(8,128)(2,1)S(1)} all-to-all(bf16[8,448,128]{2,1,0:T(8,128)(2,1)S(1)} %pad_maximum_fusion), channel_id=1, replica_groups=mesh['zy'=32,'c'=2,'r'=8] {'r'}, dimensions={0} | all-to-all | bytes 1835008 | tf_op jit(solution)/shard_map/all_to_all | solution.py:74
  38.4 0.1 slice_reduce_fusion
  38.6 0.2 compare_reduce_fusion
  38.8 0.1 slice_select_fusion
  38.9 0.1 select_reduce_fusion
  39.0 0.6 %copy.54 = bf16[32,7,128]{2,1,0:T(8,128)(2,1)} copy(bf16[32,7,128]{2,0,1:T(8,128)(2,1)S(1)} %pad_maximum_fusion.1) | data formatting | bytes 114688 | tf_op jit(solution)/shard_map/concatenate | solution.py:79
  39.7 14.9 %all-to-all-start.2 = ((bf16[32,7,128]{2,1,0:T(8,128)(2,1)}), bf16[32,7,128]{2,1,0:T(8,128)(2,1)S(1)}, u32[]{:S(2)}, u32[]{:S(2)}) async-start(bf16[32,7,128]{2,1,0:T(8,128)(2,1)} %copy.54), calls=%async_computation.2 | async-start | bytes 131072 | tf_op jit(solution)/shard_map/all_to_all | solution.py:80
  54.6 0.8 %multiply_subtract_fusion = (f32[224,128]{1,0:T(8,128)}, f32[224,128]{1,0:T(8,128)}, f32[224,128]{1,0:T(8,128)}) fusion(f32[224,128]{1,0:T(8,128)S(1)} %bitcast.76, f32[224,128]{1,0:T(8,128)S(1)} %bitcast.73, f32[224,128]{1,0:T(8,128)S(1)} %bitcast.78, f32[224,128]{1,0:T(8,128)S(1)} %bitcast.80), kind=kLoop, calls=%fused_computation.20 | loop fusion | flops 430080 | bytes 802816 | tf_op jit(solution)/shard_map/sub | solution.py:25
  55.4 0.3 convolution_convert_fusion.1
  55.6 0.1 copy.56
  55.7 0.8 %broadcast_in_dim_reshape.15 = bf16[1,1,4,28672]{3,2,1,0:T(4,128)(2,1)} reshape(bf16[4,4,56,128]{3,2,1,0:T(8,128)(2,1)S(1)} %copy.56) | data formatting | bytes 458752 | tf_op jit(solution)/shard_map/broadcast_in_dim;reshape | solution.py:115
  56.5 5.4 %all-to-all-done.2 = bf16[32,7,128]{2,1,0:T(8,128)(2,1)S(1)} async-done(((bf16[32,7,128]{2,1,0:T(8,128)(2,1)}), bf16[32,7,128]{2,1,0:T(8,128)(2,1)S(1)}, u32[]{:S(2)}, u32[]{:S(2)}) %all-to-all-start.2) | async-done | bytes 57376 | tf_op jit(solution)/shard_map/all_to_all | solution.py:80
  61.9 0.6 multiply_subtract_fusion.1
  (29 shorter events, 0.2 us)
Async XLA Ops:
  0.6 1.2 %copy-start = (bf16[1,1,64,7168]{3,2,1,0:T(8,128)(2,1)S(1)}, bf16[1,1,64,7168]{3,2,1,0:T(8,128)(2,1)}, u32[]{:S(2)}) copy-start(bf16[1,1,64,7168]{3,2,1,0:T(8,128)(2,1)} %param.14) | copy-start | bytes 2752516
  2.3 2.1 %copy-start.4 = (bf16[1,1,32,7168]{3,2,1,0:T(8,128)(2,1)S(1)}, bf16[1,1,32,7168]{3,2,1,0:T(8,128)(2,1)}, u32[]{:S(2)}) copy-start(bf16[1,1,32,7168]{3,2,1,0:T(8,128)(2,1)} %param.10) | copy-start | bytes 1376260
  2.3 9.7 %collective-permute-start = (bf16[32,7168]{1,0:T(8,128)(2,1)S(1)}, bf16[32,7168]{1,0:T(8,128)(2,1)S(1)}, u32[]{:S(2)}, u32[]{:S(2)}) collective-permute-start(bf16[32,7168]{1,0:T(8,128)(2,1)S(1)} %slice.30), channel_id=1, source_target_pairs={{0,8},{8,0},{1,9},{9,1},{2,10},{10,2},{3,11},{11,3},{4,12},{12,4},... | collective-permute-start | bytes 1376264 | tf_op jit(solution)/shard_map/ppermute | solution.py:61
  5.3 14.8 %all-to-all-start = ((bf16[8,4,7168]{2,1,0:T(4,128)(2,1)}), bf16[8,4,7168]{2,1,0:T(4,128)(2,1)S(1)}, u32[]{:S(2)}, u32[]{:S(2)}) async-start(bf16[8,4,7168]{2,1,0:T(4,128)(2,1)} %reshape_squeeze.15), calls=%async_computation | async-start | bytes 917504 | tf_op jit(solution)/shard_map/all_to_all | solution.py:50
  12.1 8.2 %copy-start.1 = (f32[1,4,7168]{2,1,0:T(4,128)S(1)}, f32[1,4,7168]{2,1,0:T(4,128)}, u32[]{:S(2)}) copy-start(f32[1,4,7168]{2,1,0:T(4,128)} %param.11) | copy-start | bytes 344068
  12.1 8.2 %copy-start.2 = (f32[1,4,7168]{2,1,0:T(4,128)S(1)}, f32[1,4,7168]{2,1,0:T(4,128)}, u32[]{:S(2)}) copy-start(f32[1,4,7168]{2,1,0:T(4,128)} %param.12) | copy-start | bytes 344068
  12.1 8.2 %copy-start.3 = (f32[1,4,7168]{2,1,0:T(4,128)S(1)}, f32[1,4,7168]{2,1,0:T(4,128)}, u32[]{:S(2)}) copy-start(f32[1,4,7168]{2,1,0:T(4,128)} %param.13) | copy-start | bytes 344068
  39.7 22.2 %all-to-all-start.2 = ((bf16[32,7,128]{2,1,0:T(8,128)(2,1)}), bf16[32,7,128]{2,1,0:T(8,128)(2,1)S(1)}, u32[]{:S(2)}, u32[]{:S(2)}) async-start(bf16[32,7,128]{2,1,0:T(8,128)(2,1)} %copy.54), calls=%async_computation.2 | async-start | bytes 131072 | tf_op jit(solution)/shard_map/all_to_all | solution.py:80
  55.3 6.6 %copy-start.5 = (f32[896]{0:T(1024)S(1)}, f32[896]{0:T(1024)}, u32[]{:S(2)}) copy-start(f32[896]{0:T(1024)} %param.15) | copy-start | bytes 10756
  55.3 6.6 %copy-start.6 = (f32[896]{0:T(1024)S(1)}, f32[896]{0:T(1024)}, u32[]{:S(2)}) copy-start(f32[896]{0:T(1024)} %param.16) | copy-start | bytes 10756
  55.4 6.6 %copy-start.7 = (f32[896]{0:T(1024)S(1)}, f32[896]{0:T(1024)}, u32[]{:S(2)}) copy-start(f32[896]{0:T(1024)} %param.17) | copy-start | bytes 10756

commit v5 on v4

--- a/solution.py
+++ b/solution.py
@@ -1,6 +1,7 @@
 import jax
 import jax.numpy as jnp
 from jax import lax
+from jax.experimental import pallas as pl
 from jax.sharding import Mesh, PartitionSpec as P
 
 
@@ -15,6 +16,8 @@
 EDP = "r"
 FIRST = 30
 MEMBERS = [(FIRST + j) % 32 for j in range(32)]
+LEAD = 2
+RANKS = [(LEAD + j) % 8 for j in range(8)]
 ABSENT = 2.0**100
 
 
@@ -34,6 +37,11 @@
     return x.reshape(56, 4, 128).transpose(1, 0, 2).reshape(4, 7168)
 
 
+def chunk_kernel(rows_ref, chunks_ref):
+    for place, rank in enumerate(RANKS):
+        chunks_ref[place] = rows_ref[4 * rank : 4 * rank + 4, :]
+
+
 def body(
     expert_grads,
     expert_param,
@@ -46,8 +54,17 @@
     writer,
     live_blocks,
 ):
-    outgoing = expert_grads[0, 0].reshape(8, 4, 7168)
-    arrived = lax.all_to_all(outgoing, EDP, split_axis=0, concat_axis=0, tiled=True)
+    outgoing = pl.pallas_call(
+        chunk_kernel,
+        grid=(2,),
+        in_specs=[pl.BlockSpec((32, 3584), lambda half: (0, half))],
+        out_specs=pl.BlockSpec((8, 4, 3584), lambda half: (0, 0, half)),
+        out_shape=jax.ShapeDtypeStruct((8, 4, 7168), jnp.bfloat16),
+        name="chunks",
+    )(expert_grads[0, 0])
+    arrived = lax.all_to_all(
+        outgoing, EDP, split_axis=0, concat_axis=0, tiled=True, axis_index_groups=[RANKS]
+    )
     expert_sum = to_tiles(arrived.astype(jnp.float32).sum(axis=0))
     state = (to_tiles(expert_param[0]), to_tiles(expert_moment[0]), to_tiles(expert_second[0]))
 
@@ -62,16 +79,19 @@
     pair = parted[:32].astype(jnp.float32) + swapped.astype(jnp.float32)
     pair = pair.astype(jnp.bfloat16).reshape(4, 8, 8, 7, 128).transpose(2, 0, 3, 1, 4)
     pair = pair.reshape(8, 224, 128)
+    pair = jnp.concatenate([pair[LEAD:], pair[:LEAD]], axis=0)
 
     expert_new, _, _ = adam_update(*state, expert_sum)
     row = lax.broadcasted_iota(jnp.int32, (224, 128), 0)
     block = (row % 4) * 56 + row // 4
     kept = jnp.where(block < live_blocks[0, 0], expert_new, 0.0).astype(jnp.bfloat16)
     rank = lax.broadcasted_iota(jnp.int32, (8, 224, 128), 0)
-    slices = jnp.where(rank == writer[0, 0, 0], kept[None], jnp.bfloat16(ABSENT))
+    slices = jnp.where((rank + LEAD) % 8 == writer[0, 0, 0], kept[None], jnp.bfloat16(ABSENT))
 
     second = jnp.concatenate([slices, pair], axis=1)
-    both = lax.all_to_all(second, EDP, split_axis=0, concat_axis=0, tiled=True)
+    both = lax.all_to_all(
+        second, EDP, split_axis=0, concat_axis=0, tiled=True, axis_index_groups=[RANKS]
+    )
     partial = both[:, 224:].astype(jnp.float32).sum(axis=0)
 
     rows = partial.reshape(4, 7, 8, 128).transpose(0, 2, 1, 3).reshape(32, 7, 128)
@@ -92,8 +112,8 @@
     )
 
     present = (received[:, 0, 0].astype(jnp.float32) < ABSENT / 2)
-    index = lax.broadcasted_iota(jnp.int32, (8, 8), 0)
-    index2 = lax.broadcasted_iota(jnp.int32, (8, 8), 1)
+    index = (lax.broadcasted_iota(jnp.int32, (8, 8), 0) + LEAD) % 8
+    index2 = (lax.broadcasted_iota(jnp.int32, (8, 8), 1) + LEAD) % 8
     before = jnp.sum(jnp.where((index2 < index) & present[None, :], 1, 0), axis=1)
     slot = lax.broadcasted_iota(jnp.int32, (4, 8), 0)
     selector = ((slot == before[None, :]) & present[None, :]).astype(jnp.bfloat16)

time: 62.9 us -> 63.4 us (level)
  the two profiles are of different devices: /device:TPU:16 before, /device:TPU:2 now
where the time goes in v5:
time: 63.4 us; the launch traced here: 63 us
  starting transfers between devices  24.8 us (39%)
  blocking collectives  17.5 us (28%)
  waiting for transfers between devices  10.2 us (16%)
  other arithmetic  2.83 us (4%)
  local copies, waits for them, and re-layouts  2.78 us (4%)
  between operations  2.22 us (4%)
  Pallas kernels  1.81 us (3%)
  matrix products  0.73 us (1%)
    all_to_all x1, blocking collectives, body(): lax.all_to_all(second, EDP, split_axis=0, concat_axis=0, tiled=True, axis...  17.5 us
    all_to_all x1, starting transfers between devices, body(): lax.all_to_all(rows, 'zy', split_axis=0, concat_axis=0, tiled=True, axis_...  14.3 us
    all_to_all x1, starting transfers between devices, body(): lax.all_to_all(outgoing, EDP, split_axis=0, concat_axis=0, tiled=True, ax...  8.6 us
    all_to_all x1, waiting for transfers between devices, body(): lax.all_to_all(outgoing, EDP, split_axis=0, concat_axis=0, tiled=True, ax...  6.63 us
    all_to_all x1, waiting for transfers between devices, body(): lax.all_to_all(rows, 'zy', split_axis=0, concat_axis=0, tiled=True, axis_...  3.61 us
    ppermute x1, starting transfers between devices, body(): swapped = lax.ppermute(parted[32:], 'c', [(0, 1), (1, 0)])  1.92 us
    pallas_call x1, Pallas kernels, body(): pl.pallas_call(chunk_kernel, grid=(2,), in_specs=[pl.BlockSpec((32, 3584)...  1.81 us
    sub x2, other arithmetic, adam_update(): master_new = master - LEARN_RATE * (direction + DECAY_RATE * master)  1.39 us
  transfers between devices with their start and end apart: 3, of which 2 were waited for; matrix products, arithmetic and copies ran while one was open for 3% of the time, Pallas kernels for 3%

profile of v5, /device:TPU:2, one launch (start us, length us, event | category | flops | bytes accessed | tf_op | source)
XLA Modules:
  0.0 63.0 jit_solution(12652424827347955536)
XLA Ops:
  0.7 1.1 %copy-done = bf16[1,1,64,7168]{3,2,1,0:T(8,128)(2,1)S(1)} copy-done((bf16[1,1,64,7168]{3,2,1,0:T(8,128)(2,1)S(1)}, bf16[1,1,64,7168]{3,2,1,0:T(8,128)(2,1)}, u32[]{:S(2)}) %copy-start) | copy-done | bytes 917528
  1.8 0.5 convolution_convert_fusion
  2.3 1.9 %collective-permute-start = (bf16[32,7168]{1,0:T(8,128)(2,1)S(1)}, bf16[32,7168]{1,0:T(8,128)(2,1)S(1)}, u32[]{:S(2)}, u32[]{:S(2)}) collective-permute-start(bf16[32,7168]{1,0:T(8,128)(2,1)S(1)} %slice.46), channel_id=1, source_target_pairs={{0,8},{8,0},{1,9},{9,1},{2,10},{10,2},{3,11},{11,3},{4,12},{12,4},... | collective-permute-start | bytes 1376264 | tf_op jit(solution)/shard_map/ppermute | solution.py:78
  4.3 1.8 %chunks.1 = bf16[8,4,7168]{2,1,0:T(4,128)(2,1)} custom-call(bf16[32,7168]{1,0:T(8,128)(2,1)} %bitcast.83), custom_call_target="tpu_custom_call" | custom-call | tf_op jit(solution)/shard_map/chunks/pallas_call | solution.py:57
  6.1 8.6 %all-to-all-start = ((bf16[8,4,7168]{2,1,0:T(4,128)(2,1)}), bf16[8,4,7168]{2,1,0:T(4,128)(2,1)S(1)}, u32[]{:S(2)}, u32[]{:S(2)}) async-start(bf16[8,4,7168]{2,1,0:T(4,128)(2,1)} %chunks.1), calls=%async_computation | async-start | bytes 917504 | tf_op jit(solution)/shard_map/all_to_all | solution.py:65
  16.0 0.1 add_convert_fusion
  16.3 6.6 %all-to-all-done = bf16[8,4,7168]{2,1,0:T(4,128)(2,1)S(1)} async-done(((bf16[8,4,7168]{2,1,0:T(4,128)(2,1)}), bf16[8,4,7168]{2,1,0:T(4,128)(2,1)S(1)}, u32[]{:S(2)}, u32[]{:S(2)}) %all-to-all-start) | async-done | bytes 458784 | tf_op jit(solution)/shard_map/all_to_all | solution.py:65
  22.9 0.2 convert_reduce_fusion
  23.1 0.2 select_convert_fusion
  23.4 0.1 fusion.1
  23.5 0.1 maximum_maximum_fusion
  23.6 17.5 %all_to_all.15 = bf16[8,448,128]{2,1,0:T(8,128)(2,1)S(1)} all-to-all(bf16[8,448,128]{2,1,0:T(8,128)(2,1)S(1)} %maximum_maximum_fusion), channel_id=1, replica_groups={{2,3,4,5,6,7,0,1},{10,11,12,13,14,15,8,9},{18,19,20,21,22,23,16,17},{26..., dimensions={0} | all-to-all | bytes 1835008 | tf_op jit(solution)/shard_map/all_to_all | solution.py:92
  41.1 0.1 slice_reduce_fusion
  41.3 0.2 compare_reduce_fusion
  41.5 0.1 slice_select_fusion
  41.6 0.2 select_reduce_fusion
  41.8 0.7 %copy.60 = bf16[32,7,128]{2,1,0:T(8,128)(2,1)} copy(bf16[32,7,128]{2,0,1:T(8,128)(2,1)S(1)} %pad_maximum_fusion) | data formatting | bytes 114688 | tf_op jit(solution)/shard_map/concatenate | solution.py:99
  42.5 14.3 %all-to-all-start.2 = ((bf16[32,7,128]{2,1,0:T(8,128)(2,1)}), bf16[32,7,128]{2,1,0:T(8,128)(2,1)S(1)}, u32[]{:S(2)}, u32[]{:S(2)}) async-start(bf16[32,7,128]{2,1,0:T(8,128)(2,1)} %copy.60), calls=%async_computation.2 | async-start | bytes 131072 | tf_op jit(solution)/shard_map/all_to_all | solution.py:100
  56.8 0.8 %multiply_subtract_fusion = (f32[224,128]{1,0:T(8,128)}, f32[224,128]{1,0:T(8,128)}, f32[224,128]{1,0:T(8,128)}) fusion(f32[224,128]{1,0:T(8,128)S(1)} %bitcast.78, f32[224,128]{1,0:T(8,128)S(1)} %bitcast.74, f32[224,128]{1,0:T(8,128)S(1)} %bitcast.80, f32[224,128]{1,0:T(8,128)S(1)} %bitcast.82), kind=kLoop, calls=%fused_computation.21 | loop fusion | flops 430080 | bytes 802816 | tf_op jit(solution)/shard_map/sub | solution.py:28
  57.6 0.3 convolution_convert_fusion.1
  57.9 0.1 copy.62
  57.9 0.8 %broadcast_in_dim_reshape.15 = bf16[1,1,4,28672]{3,2,1,0:T(4,128)(2,1)} reshape(bf16[4,4,56,128]{3,2,1,0:T(8,128)(2,1)S(1)} %copy.62) | data formatting | bytes 458752 | tf_op jit(solution)/shard_map/broadcast_in_dim;reshape | solution.py:135
  58.7 3.6 %all-to-all-done.2 = bf16[32,7,128]{2,1,0:T(8,128)(2,1)S(1)} async-done(((bf16[32,7,128]{2,1,0:T(8,128)(2,1)}), bf16[32,7,128]{2,1,0:T(8,128)(2,1)S(1)}, u32[]{:S(2)}, u32[]{:S(2)}) %all-to-all-start.2) | async-done | bytes 57376 | tf_op jit(solution)/shard_map/all_to_all | solution.py:100
  62.4 0.6 multiply_subtract_fusion.1
  (31 shorter events, 0.3 us)
Async XLA Ops:
  0.6 1.2 %copy-start = (bf16[1,1,64,7168]{3,2,1,0:T(8,128)(2,1)S(1)}, bf16[1,1,64,7168]{3,2,1,0:T(8,128)(2,1)}, u32[]{:S(2)}) copy-start(bf16[1,1,64,7168]{3,2,1,0:T(8,128)(2,1)} %param.14) | copy-start | bytes 2752516
  2.3 13.7 %collective-permute-start = (bf16[32,7168]{1,0:T(8,128)(2,1)S(1)}, bf16[32,7168]{1,0:T(8,128)(2,1)S(1)}, u32[]{:S(2)}, u32[]{:S(2)}) collective-permute-start(bf16[32,7168]{1,0:T(8,128)(2,1)S(1)} %slice.46), channel_id=1, source_target_pairs={{0,8},{8,0},{1,9},{9,1},{2,10},{10,2},{3,11},{11,3},{4,12},{12,4},... | collective-permute-start | bytes 1376264 | tf_op jit(solution)/shard_map/ppermute | solution.py:78
  6.1 16.9 %all-to-all-start = ((bf16[8,4,7168]{2,1,0:T(4,128)(2,1)}), bf16[8,4,7168]{2,1,0:T(4,128)(2,1)S(1)}, u32[]{:S(2)}, u32[]{:S(2)}) async-start(bf16[8,4,7168]{2,1,0:T(4,128)(2,1)} %chunks.1), calls=%async_computation | async-start | bytes 917504 | tf_op jit(solution)/shard_map/all_to_all | solution.py:65
  16.2 6.9 %copy-start.1 = (f32[1,4,7168]{2,1,0:T(4,128)S(1)}, f32[1,4,7168]{2,1,0:T(4,128)}, u32[]{:S(2)}) copy-start(f32[1,4,7168]{2,1,0:T(4,128)} %param.11) | copy-start | bytes 344068
  16.2 6.9 %copy-start.2 = (f32[1,4,7168]{2,1,0:T(4,128)S(1)}, f32[1,4,7168]{2,1,0:T(4,128)}, u32[]{:S(2)}) copy-start(f32[1,4,7168]{2,1,0:T(4,128)} %param.12) | copy-start | bytes 344068
  16.2 6.9 %copy-start.3 = (f32[1,4,7168]{2,1,0:T(4,128)S(1)}, f32[1,4,7168]{2,1,0:T(4,128)}, u32[]{:S(2)}) copy-start(f32[1,4,7168]{2,1,0:T(4,128)} %param.13) | copy-start | bytes 344068
  42.5 19.8 %all-to-all-start.2 = ((bf16[32,7,128]{2,1,0:T(8,128)(2,1)}), bf16[32,7,128]{2,1,0:T(8,128)(2,1)S(1)}, u32[]{:S(2)}, u32[]{:S(2)}) async-start(bf16[32,7,128]{2,1,0:T(8,128)(2,1)} %copy.60), calls=%async_computation.2 | async-start | bytes 131072 | tf_op jit(solution)/shard_map/all_to_all | solution.py:100
  57.6 4.8 %copy-start.4 = (f32[896]{0:T(1024)S(1)}, f32[896]{0:T(1024)}, u32[]{:S(2)}) copy-start(f32[896]{0:T(1024)} %param.15) | copy-start | bytes 10756
  57.6 4.8 %copy-start.5 = (f32[896]{0:T(1024)S(1)}, f32[896]{0:T(1024)}, u32[]{:S(2)}) copy-start(f32[896]{0:T(1024)} %param.16) | copy-start | bytes 10756
  57.6 4.8 %copy-start.6 = (f32[896]{0:T(1024)S(1)}, f32[896]{0:T(1024)}, u32[]{:S(2)}) copy-start(f32[896]{0:T(1024)} %param.17) | copy-start | bytes 10756

commit v6 on v5

--- a/solution.py
+++ b/solution.py
@@ -17,7 +17,7 @@
 FIRST = 30
 MEMBERS = [(FIRST + j) % 32 for j in range(32)]
 LEAD = 2
-RANKS = [(LEAD + j) % 8 for j in range(8)]
+RANKS = [j % 2 * 4 + (LEAD + j // 2) % 4 for j in range(8)]
 ABSENT = 2.0**100
 
 
@@ -35,6 +35,10 @@
 
 def from_tiles(x):
     return x.reshape(56, 4, 128).transpose(1, 0, 2).reshape(4, 7168)
+
+
+def rank_at(place):
+    return place % 2 * 4 + (LEAD + place // 2) % 4
 
 
 def chunk_kernel(rows_ref, chunks_ref):
@@ -77,16 +81,16 @@
     parted = parted.astype(jnp.bfloat16)
     swapped = lax.ppermute(parted[32:], "c", [(0, 1), (1, 0)])
     pair = parted[:32].astype(jnp.float32) + swapped.astype(jnp.float32)
-    pair = pair.astype(jnp.bfloat16).reshape(4, 8, 8, 7, 128).transpose(2, 0, 3, 1, 4)
+    pair = pair.astype(jnp.bfloat16).reshape(4, 8, 2, 4, 7, 128).transpose(3, 2, 0, 4, 1, 5)
     pair = pair.reshape(8, 224, 128)
-    pair = jnp.concatenate([pair[LEAD:], pair[:LEAD]], axis=0)
+    pair = jnp.concatenate([pair[2 * LEAD :], pair[: 2 * LEAD]], axis=0)
 
     expert_new, _, _ = adam_update(*state, expert_sum)
     row = lax.broadcasted_iota(jnp.int32, (224, 128), 0)
     block = (row % 4) * 56 + row // 4
     kept = jnp.where(block < live_blocks[0, 0], expert_new, 0.0).astype(jnp.bfloat16)
     rank = lax.broadcasted_iota(jnp.int32, (8, 224, 128), 0)
-    slices = jnp.where((rank + LEAD) % 8 == writer[0, 0, 0], kept[None], jnp.bfloat16(ABSENT))
+    slices = jnp.where(rank_at(rank) == writer[0, 0, 0], kept[None], jnp.bfloat16(ABSENT))
 
     second = jnp.concatenate([slices, pair], axis=1)
     both = lax.all_to_all(
@@ -95,12 +99,11 @@
     partial = both[:, 224:].astype(jnp.float32).sum(axis=0)
 
     rows = partial.reshape(4, 7, 8, 128).transpose(0, 2, 1, 3).reshape(32, 7, 128)
-    rows = rows.astype(jnp.bfloat16)
     rows = jnp.concatenate([rows[FIRST:], rows[:FIRST]], axis=0)
     last = lax.all_to_all(
         rows, "zy", split_axis=0, concat_axis=0, tiled=True, axis_index_groups=[MEMBERS]
     )
-    dense_sum = last.astype(jnp.float32).sum(axis=0).reshape(-1)
+    dense_sum = last.sum(axis=0).reshape(-1)
 
     state, expert_sum, both, _ = lax.optimization_barrier((state, expert_sum, both, rows))
     received = both[:, :224]
@@ -112,8 +115,8 @@
     )
 
     present = (received[:, 0, 0].astype(jnp.float32) < ABSENT / 2)
-    index = (lax.broadcasted_iota(jnp.int32, (8, 8), 0) + LEAD) % 8
-    index2 = (lax.broadcasted_iota(jnp.int32, (8, 8), 1) + LEAD) % 8
+    index = rank_at(lax.broadcasted_iota(jnp.int32, (8, 8), 0))
+    index2 = rank_at(lax.broadcasted_iota(jnp.int32, (8, 8), 1))
     before = jnp.sum(jnp.where((index2 < index) & present[None, :], 1, 0), axis=1)
     slot = lax.broadcasted_iota(jnp.int32, (4, 8), 0)
     selector = ((slot == before[None, :]) & present[None, :]).astype(jnp.bfloat16)

time: 63.4 us -> 59.8 us (0.943)
  waiting for transfers between devices: 10.2 us -> 7.37 us
  local copies, waits for them, and re-layouts: 2.78 us -> 1.73 us
  starting transfers between devices: 24.8 us -> 25.7 us
    all_to_all x1, waiting for transfers between devices: 6.63 us -> 2.68 us  [body(): lax.all_to_all(outgoing, EDP, split_axis=0, concat_axis=0, tiled=True, ax...]
    unnamed x14, local copies, waits for them, and re-layouts: 1.16 us -> 0.05 us
    all_to_all x1, starting transfers between devices: 14.3 us -> 15.2 us  [body(): lax.all_to_all(rows, 'zy', split_axis=0, concat_axis=0, tiled=True, axis_...]
    all_to_all x1, waiting for transfers between devices: 3.61 us -> 4.27 us  [body(): lax.all_to_all(rows, 'zy', split_axis=0, concat_axis=0, tiled=True, axis_...]
  transfers between devices with their start and end apart: 3 -> 3, of which waited for: 2 -> 3; matrix products, arithmetic and copies ran while one was open for 3% -> 4% of each run, Pallas kernels for 3% -> 0%
where the time goes in v6:
time: 59.8 us; the launch traced here: 59.5 us
  starting transfers between devices  25.7 us (43%)
  blocking collectives  17 us (28%)
  waiting for transfers between devices  7.37 us (12%)
  other arithmetic  2.86 us (5%)
  between operations  2.21 us (4%)
  Pallas kernels  1.89 us (3%)
  local copies, waits for them, and re-layouts  1.73 us (3%)
  matrix products  0.73 us (1%)
    all_to_all x1, blocking collectives, body(): lax.all_to_all(second, EDP, split_axis=0, concat_axis=0, tiled=True, axis...  17 us
    all_to_all x1, starting transfers between devices, body(): lax.all_to_all(rows, 'zy', split_axis=0, concat_axis=0, tiled=True, axis_...  15.2 us
    all_to_all x1, starting transfers between devices, body(): lax.all_to_all(outgoing, EDP, split_axis=0, concat_axis=0, tiled=True, ax...  8.62 us
    all_to_all x1, waiting for transfers between devices, body(): lax.all_to_all(rows, 'zy', split_axis=0, concat_axis=0, tiled=True, axis_...  4.27 us
    all_to_all x1, waiting for transfers between devices, body(): lax.all_to_all(outgoing, EDP, split_axis=0, concat_axis=0, tiled=True, ax...  2.68 us
    ppermute x1, starting transfers between devices, body(): swapped = lax.ppermute(parted[32:], 'c', [(0, 1), (1, 0)])  1.92 us
    pallas_call x1, Pallas kernels, body(): pl.pallas_call(chunk_kernel, grid=(2,), in_specs=[pl.BlockSpec((32, 3584)...  1.89 us
    sub x2, other arithmetic, adam_update(): master_new = master - LEARN_RATE * (direction + DECAY_RATE * master)  1.39 us
  transfers between devices with their start and end apart: 3, of which 3 were waited for; matrix products, arithmetic and copies ran while one was open for 4% of the time, Pallas kernels for 0%

profile of v6, /device:TPU:2, one launch (start us, length us, event | category | flops | bytes accessed | tf_op | source)
XLA Modules:
  0.0 59.5 jit_solution(3116541119345580400)
XLA Ops:
  0.6 1.9 %chunks.1 = bf16[8,4,7168]{2,1,0:T(4,128)(2,1)} custom-call(bf16[32,7168]{1,0:T(8,128)(2,1)} %bitcast.86), custom_call_target="tpu_custom_call" | custom-call | tf_op jit(solution)/shard_map/chunks/pallas_call | solution.py:61
  2.5 8.6 %all-to-all-start = ((bf16[8,4,7168]{2,1,0:T(4,128)(2,1)}), bf16[8,4,7168]{2,1,0:T(4,128)(2,1)S(1)}, u32[]{:S(2)}, u32[]{:S(2)}) async-start(bf16[8,4,7168]{2,1,0:T(4,128)(2,1)} %chunks.1), calls=%async_computation | async-start | bytes 917504 | tf_op jit(solution)/shard_map/all_to_all | solution.py:69
  11.2 0.5 convolution_convert_fusion
  11.7 1.9 %collective-permute-start = (bf16[32,7168]{1,0:T(8,128)(2,1)S(1)}, bf16[32,7168]{1,0:T(8,128)(2,1)S(1)}, u32[]{:S(2)}, u32[]{:S(2)}) collective-permute-start(bf16[32,7168]{1,0:T(8,128)(2,1)S(1)} %slice.46), channel_id=1, source_target_pairs={{0,8},{8,0},{1,9},{9,1},{2,10},{10,2},{3,11},{11,3},{4,12},{12,4},... | collective-permute-start | bytes 1376264 | tf_op jit(solution)/shard_map/ppermute | solution.py:82
  15.0 0.4 collective-permute-done
  15.4 0.1 add_convert_fusion
  15.6 2.7 %all-to-all-done = bf16[8,4,7168]{2,1,0:T(4,128)(2,1)S(1)} async-done(((bf16[8,4,7168]{2,1,0:T(4,128)(2,1)}), bf16[8,4,7168]{2,1,0:T(4,128)(2,1)S(1)}, u32[]{:S(2)}, u32[]{:S(2)}) %all-to-all-start) | async-done | bytes 458784 | tf_op jit(solution)/shard_map/all_to_all | solution.py:69
  18.3 0.2 convert_reduce_fusion.1
  18.5 0.2 select_convert_fusion
  18.8 0.2 fusion.4
  19.0 0.1 maximum_maximum_fusion
  19.0 17.0 %all_to_all.15 = bf16[8,448,128]{2,1,0:T(8,128)(2,1)S(1)} all-to-all(bf16[8,448,128]{2,1,0:T(8,128)(2,1)S(1)} %maximum_maximum_fusion), channel_id=1, replica_groups={{2,6,3,7,0,4,1,5},{10,14,11,15,8,12,9,13},{18,22,19,23,16,20,17,21},{26..., dimensions={0} | all-to-all | bytes 1835008 | tf_op jit(solution)/shard_map/all_to_all | solution.py:96
  36.0 0.1 convert_reduce_fusion
  36.1 0.7 %copy.47 = f32[32,7,128]{2,1,0:T(8,128)} copy(f32[32,7,128]{2,0,1:T(8,128)S(1)} %pad_maximum_fusion) | data formatting | bytes 229376 | tf_op jit(solution)/shard_map/concatenate | solution.py:102
  36.8 0.2 compare_reduce_fusion
  37.1 0.1 slice_select_fusion
  37.2 0.2 select_reduce_fusion
  37.4 15.2 %all-to-all-start.2 = ((f32[32,7,128]{2,1,0:T(8,128)}), f32[32,7,128]{2,1,0:T(8,128)S(1)}, u32[]{:S(2)}, u32[]{:S(2)}) async-start(f32[32,7,128]{2,1,0:T(8,128)} %copy.47), calls=%async_computation.2 | async-start | bytes 262144 | tf_op jit(solution)/shard_map/all_to_all | solution.py:103
  52.6 0.3 convolution_convert_fusion.1
  52.9 0.1 copy.49
  53.0 0.8 %broadcast_in_dim_reshape.15 = bf16[1,1,4,28672]{3,2,1,0:T(4,128)(2,1)} reshape(bf16[4,4,56,128]{3,2,1,0:T(8,128)(2,1)S(1)} %copy.49) | data formatting | bytes 458752 | tf_op jit(solution)/shard_map/broadcast_in_dim;reshape | solution.py:138
  53.7 0.8 %multiply_subtract_fusion = (f32[224,128]{1,0:T(8,128)}, f32[224,128]{1,0:T(8,128)}, f32[224,128]{1,0:T(8,128)}) fusion(f32[224,128]{1,0:T(8,128)S(1)} %bitcast.81, f32[224,128]{1,0:T(8,128)S(1)} %bitcast.74, f32[224,128]{1,0:T(8,128)S(1)} %bitcast.83, f32[224,128]{1,0:T(8,128)S(1)} %bitcast.85), kind=kLoop, calls=%fused_computation.28 | loop fusion | flops 430080 | bytes 802816 | tf_op jit(solution)/shard_map/sub | solution.py:28
  54.5 4.3 %all-to-all-done.2 = f32[32,7,128]{2,1,0:T(8,128)S(1)} async-done(((f32[32,7,128]{2,1,0:T(8,128)}), f32[32,7,128]{2,1,0:T(8,128)S(1)}, u32[]{:S(2)}, u32[]{:S(2)}) %all-to-all-start.2) | async-done | bytes 114720 | tf_op jit(solution)/shard_map/all_to_all | solution.py:103
  58.8 0.6 %multiply_subtract_fusion.1 = (f32[896]{0:T(1024)}, f32[896]{0:T(1024)}, f32[896]{0:T(1024)}) fusion(f32[896]{0:T(1024)S(1)} %copy-done.4, f32[7,128]{1,0:T(8,128)S(1)} %reduce_sum.38, f32[896]{0:T(1024)S(1)} %copy-done.5, f32[896]{0:T(1024)S(1)} %copy-done.6), kind=kLoop, calls=%fused_computation.55 | loop fusion | flops 13440 | bytes 25088 | tf_op jit(solution)/shard_map/sub | solution.py:28
  (30 shorter events, 0.3 us)
Async XLA Ops:
  0.6 10.5 %copy-start = (bf16[1,1,64,7168]{3,2,1,0:T(8,128)(2,1)S(1)}, bf16[1,1,64,7168]{3,2,1,0:T(8,128)(2,1)}, u32[]{:S(2)}) copy-start(bf16[1,1,64,7168]{3,2,1,0:T(8,128)(2,1)} %param.14) | copy-start | bytes 2752516
  2.5 15.8 %all-to-all-start = ((bf16[8,4,7168]{2,1,0:T(4,128)(2,1)}), bf16[8,4,7168]{2,1,0:T(4,128)(2,1)S(1)}, u32[]{:S(2)}, u32[]{:S(2)}) async-start(bf16[8,4,7168]{2,1,0:T(4,128)(2,1)} %chunks.1), calls=%async_computation | async-start | bytes 917504 | tf_op jit(solution)/shard_map/all_to_all | solution.py:69
  11.7 3.7 %collective-permute-start = (bf16[32,7168]{1,0:T(8,128)(2,1)S(1)}, bf16[32,7168]{1,0:T(8,128)(2,1)S(1)}, u32[]{:S(2)}, u32[]{:S(2)}) collective-permute-start(bf16[32,7168]{1,0:T(8,128)(2,1)S(1)} %slice.46), channel_id=1, source_target_pairs={{0,8},{8,0},{1,9},{9,1},{2,10},{10,2},{3,11},{11,3},{4,12},{12,4},... | collective-permute-start | bytes 1376264 | tf_op jit(solution)/shard_map/ppermute | solution.py:82
  15.6 3.0 %copy-start.1 = (f32[1,4,7168]{2,1,0:T(4,128)S(1)}, f32[1,4,7168]{2,1,0:T(4,128)}, u32[]{:S(2)}) copy-start(f32[1,4,7168]{2,1,0:T(4,128)} %param.11) | copy-start | bytes 344068
  15.6 3.0 %copy-start.2 = (f32[1,4,7168]{2,1,0:T(4,128)S(1)}, f32[1,4,7168]{2,1,0:T(4,128)}, u32[]{:S(2)}) copy-start(f32[1,4,7168]{2,1,0:T(4,128)} %param.12) | copy-start | bytes 344068
  15.6 3.0 %copy-start.3 = (f32[1,4,7168]{2,1,0:T(4,128)S(1)}, f32[1,4,7168]{2,1,0:T(4,128)}, u32[]{:S(2)}) copy-start(f32[1,4,7168]{2,1,0:T(4,128)} %param.13) | copy-start | bytes 344068
  37.4 21.4 %all-to-all-start.2 = ((f32[32,7,128]{2,1,0:T(8,128)}), f32[32,7,128]{2,1,0:T(8,128)S(1)}, u32[]{:S(2)}, u32[]{:S(2)}) async-start(f32[32,7,128]{2,1,0:T(8,128)} %copy.47), calls=%async_computation.2 | async-start | bytes 262144 | tf_op jit(solution)/shard_map/all_to_all | solution.py:103
  52.9 6.0 %copy-start.4 = (f32[896]{0:T(1024)S(1)}, f32[896]{0:T(1024)}, u32[]{:S(2)}) copy-start(f32[896]{0:T(1024)} %param.15) | copy-start | bytes 10756
  52.9 6.0 %copy-start.5 = (f32[896]{0:T(1024)S(1)}, f32[896]{0:T(1024)}, u32[]{:S(2)}) copy-start(f32[896]{0:T(1024)} %param.16) | copy-start | bytes 10756
  52.9 5.9 %copy-start.6 = (f32[896]{0:T(1024)S(1)}, f32[896]{0:T(1024)}, u32[]{:S(2)}) copy-start(f32[896]{0:T(1024)} %param.17) | copy-start | bytes 10756

commit v7 on v6

--- a/solution.py
+++ b/solution.py
@@ -14,9 +14,9 @@
 SECOND_BIAS = 1.0 - BETA_SECOND**10
 EP = ("zy", "c")
 EDP = "r"
-FIRST = 30
+FIRST = 26
 MEMBERS = [(FIRST + j) % 32 for j in range(32)]
-LEAD = 2
+LEAD = 3
 RANKS = [j % 2 * 4 + (LEAD + j // 2) % 4 for j in range(8)]
 ABSENT = 2.0**100
 
@@ -99,11 +99,12 @@
     partial = both[:, 224:].astype(jnp.float32).sum(axis=0)
 
     rows = partial.reshape(4, 7, 8, 128).transpose(0, 2, 1, 3).reshape(32, 7, 128)
+    rows = rows.astype(jnp.bfloat16)
     rows = jnp.concatenate([rows[FIRST:], rows[:FIRST]], axis=0)
     last = lax.all_to_all(
         rows, "zy", split_axis=0, concat_axis=0, tiled=True, axis_index_groups=[MEMBERS]
     )
-    dense_sum = last.sum(axis=0).reshape(-1)
+    dense_sum = last.astype(jnp.float32).sum(axis=0).reshape(-1)
 
     state, expert_sum, both, _ = lax.optimization_barrier((state, expert_sum, both, rows))
     received = both[:, :224]

time: 59.8 us -> 57.5 us (0.962)
  the two profiles are of different devices: /device:TPU:2 before, /device:TPU:16 now
where the time goes in v7:
time: 57.5 us; the launch traced here: 57.1 us
  starting transfers between devices  24.2 us (42%)
  blocking collectives  16.2 us (28%)
  waiting for transfers between devices  7.39 us (13%)
  other arithmetic  2.87 us (5%)
  between operations  2.2 us (4%)
  Pallas kernels  1.91 us (3%)
  local copies, waits for them, and re-layouts  1.66 us (3%)
  matrix products  0.73 us (1%)
    all_to_all x1, blocking collectives, body(): lax.all_to_all(second, EDP, split_axis=0, concat_axis=0, tiled=True, axis...  16.2 us
    all_to_all x1, starting transfers between devices, body(): lax.all_to_all(rows, 'zy', split_axis=0, concat_axis=0, tiled=True, axis_...  15.8 us
    all_to_all x1, starting transfers between devices, body(): lax.all_to_all(outgoing, EDP, split_axis=0, concat_axis=0, tiled=True, ax...  6.45 us
    all_to_all x1, waiting for transfers between devices, body(): lax.all_to_all(rows, 'zy', split_axis=0, concat_axis=0, tiled=True, axis_...  4.53 us
    all_to_all x1, waiting for transfers between devices, body(): lax.all_to_all(outgoing, EDP, split_axis=0, concat_axis=0, tiled=True, ax...  2.45 us
    ppermute x1, starting transfers between devices, body(): swapped = lax.ppermute(parted[32:], 'c', [(0, 1), (1, 0)])  1.92 us
    pallas_call x1, Pallas kernels, body(): pl.pallas_call(chunk_kernel, grid=(2,), in_specs=[pl.BlockSpec((32, 3584)...  1.91 us
    sub x2, other arithmetic, adam_update(): master_new = master - LEARN_RATE * (direction + DECAY_RATE * master)  1.39 us
  transfers between devices with their start and end apart: 3, of which 3 were waited for; matrix products, arithmetic and copies ran while one was open for 5% of the time, Pallas kernels for 0%

profile of v7, /device:TPU:16, one launch (start us, length us, event | category | flops | bytes accessed | tf_op | source)
XLA Modules:
  0.0 57.1 jit_solution(11226208160591110589)
XLA Ops:
  0.6 1.9 %chunks.1 = bf16[8,4,7168]{2,1,0:T(4,128)(2,1)} custom-call(bf16[32,7168]{1,0:T(8,128)(2,1)} %bitcast.85), custom_call_target="tpu_custom_call" | custom-call | tf_op jit(solution)/shard_map/chunks/pallas_call | solution.py:61
  2.6 6.4 %all-to-all-start = ((bf16[8,4,7168]{2,1,0:T(4,128)(2,1)}), bf16[8,4,7168]{2,1,0:T(4,128)(2,1)S(1)}, u32[]{:S(2)}, u32[]{:S(2)}) async-start(bf16[8,4,7168]{2,1,0:T(4,128)(2,1)} %chunks.1), calls=%async_computation | async-start | bytes 917504 | tf_op jit(solution)/shard_map/all_to_all | solution.py:69
  9.0 0.5 convolution_convert_fusion
  9.5 1.9 %collective-permute-start = (bf16[32,7168]{1,0:T(8,128)(2,1)S(1)}, bf16[32,7168]{1,0:T(8,128)(2,1)S(1)}, u32[]{:S(2)}, u32[]{:S(2)}) collective-permute-start(bf16[32,7168]{1,0:T(8,128)(2,1)S(1)} %slice.46), channel_id=1, source_target_pairs={{0,8},{8,0},{1,9},{9,1},{2,10},{10,2},{3,11},{11,3},{4,12},{12,4},... | collective-permute-start | bytes 1376264 | tf_op jit(solution)/shard_map/ppermute | solution.py:82
  12.8 0.4 collective-permute-done
  13.3 0.1 add_convert_fusion
  13.5 2.4 %all-to-all-done = bf16[8,4,7168]{2,1,0:T(4,128)(2,1)S(1)} async-done(((bf16[8,4,7168]{2,1,0:T(4,128)(2,1)}), bf16[8,4,7168]{2,1,0:T(4,128)(2,1)S(1)}, u32[]{:S(2)}, u32[]{:S(2)}) %all-to-all-start) | async-done | bytes 458784 | tf_op jit(solution)/shard_map/all_to_all | solution.py:69
  15.9 0.2 convert_reduce_fusion
  16.2 0.2 select_convert_fusion
  16.4 0.2 fusion.4
  16.6 0.1 maximum_maximum_fusion
  16.7 16.2 %all_to_all.15 = bf16[8,448,128]{2,1,0:T(8,128)(2,1)S(1)} all-to-all(bf16[8,448,128]{2,1,0:T(8,128)(2,1)S(1)} %maximum_maximum_fusion), channel_id=1, replica_groups={{3,7,0,4,1,5,2,6},{11,15,8,12,9,13,10,14},{19,23,16,20,17,21,18,22},{27..., dimensions={0} | all-to-all | bytes 1835008 | tf_op jit(solution)/shard_map/all_to_all | solution.py:96
  32.9 0.1 slice_reduce_fusion
  33.0 0.7 %copy.47 = bf16[32,7,128]{2,1,0:T(8,128)(2,1)} copy(bf16[32,7,128]{2,0,1:T(8,128)(2,1)S(1)} %pad_maximum_fusion) | data formatting | bytes 114688 | tf_op jit(solution)/shard_map/concatenate | solution.py:103
  33.7 0.2 compare_reduce_fusion
  33.9 0.1 slice_select_fusion
  34.0 0.2 select_reduce_fusion
  34.2 15.8 %all-to-all-start.2 = ((bf16[32,7,128]{2,1,0:T(8,128)(2,1)}), bf16[32,7,128]{2,1,0:T(8,128)(2,1)S(1)}, u32[]{:S(2)}, u32[]{:S(2)}) async-start(bf16[32,7,128]{2,1,0:T(8,128)(2,1)} %copy.47), calls=%async_computation.2 | async-start | bytes 131072 | tf_op jit(solution)/shard_map/all_to_all | solution.py:104
  50.0 0.8 %multiply_subtract_fusion = (f32[224,128]{1,0:T(8,128)}, f32[224,128]{1,0:T(8,128)}, f32[224,128]{1,0:T(8,128)}) fusion(f32[224,128]{1,0:T(8,128)S(1)} %bitcast.80, f32[224,128]{1,0:T(8,128)S(1)} %bitcast.76, f32[224,128]{1,0:T(8,128)S(1)} %bitcast.82, f32[224,128]{1,0:T(8,128)S(1)} %bitcast.84), kind=kLoop, calls=%fused_computation.27 | loop fusion | flops 430080 | bytes 802816 | tf_op jit(solution)/shard_map/sub | solution.py:28
  50.8 0.3 convolution_convert_fusion.1
  51.1 0.1 copy.49
  51.2 0.8 %broadcast_in_dim_reshape.15 = bf16[1,1,4,28672]{3,2,1,0:T(4,128)(2,1)} reshape(bf16[4,4,56,128]{3,2,1,0:T(8,128)(2,1)S(1)} %copy.49) | data formatting | bytes 458752 | tf_op jit(solution)/shard_map/broadcast_in_dim;reshape | solution.py:139
  51.9 4.5 %all-to-all-done.2 = bf16[32,7,128]{2,1,0:T(8,128)(2,1)S(1)} async-done(((bf16[32,7,128]{2,1,0:T(8,128)(2,1)}), bf16[32,7,128]{2,1,0:T(8,128)(2,1)S(1)}, u32[]{:S(2)}, u32[]{:S(2)}) %all-to-all-start.2) | async-done | bytes 57376 | tf_op jit(solution)/shard_map/all_to_all | solution.py:104
  56.5 0.6 %multiply_subtract_fusion.1 = (f32[896]{0:T(1024)}, f32[896]{0:T(1024)}, f32[896]{0:T(1024)}) fusion(f32[896]{0:T(1024)S(1)} %copy-done.4, f32[7,128]{1,0:T(8,128)S(1)} %convert_reduce_fusion.1, f32[896]{0:T(1024)S(1)} %copy-done.5, f32[896]{0:T(1024)S(1)} %copy-done.6), kind=kLoop, calls=%fused_computation.56 | loop fusion | flops 13440 | bytes 25088 | tf_op jit(solution)/shard_map/sub | solution.py:28
  (31 shorter events, 0.3 us)
Async XLA Ops:
  0.6 8.4 %copy-start = (bf16[1,1,64,7168]{3,2,1,0:T(8,128)(2,1)S(1)}, bf16[1,1,64,7168]{3,2,1,0:T(8,128)(2,1)}, u32[]{:S(2)}) copy-start(bf16[1,1,64,7168]{3,2,1,0:T(8,128)(2,1)} %param.14) | copy-start | bytes 2752516
  2.6 13.4 %all-to-all-start = ((bf16[8,4,7168]{2,1,0:T(4,128)(2,1)}), bf16[8,4,7168]{2,1,0:T(4,128)(2,1)S(1)}, u32[]{:S(2)}, u32[]{:S(2)}) async-start(bf16[8,4,7168]{2,1,0:T(4,128)(2,1)} %chunks.1), calls=%async_computation | async-start | bytes 917504 | tf_op jit(solution)/shard_map/all_to_all | solution.py:69
  9.5 3.7 %collective-permute-start = (bf16[32,7168]{1,0:T(8,128)(2,1)S(1)}, bf16[32,7168]{1,0:T(8,128)(2,1)S(1)}, u32[]{:S(2)}, u32[]{:S(2)}) collective-permute-start(bf16[32,7168]{1,0:T(8,128)(2,1)S(1)} %slice.46), channel_id=1, source_target_pairs={{0,8},{8,0},{1,9},{9,1},{2,10},{10,2},{3,11},{11,3},{4,12},{12,4},... | collective-permute-start | bytes 1376264 | tf_op jit(solution)/shard_map/ppermute | solution.py:82
  13.4 2.7 %copy-start.1 = (f32[1,4,7168]{2,1,0:T(4,128)S(1)}, f32[1,4,7168]{2,1,0:T(4,128)}, u32[]{:S(2)}) copy-start(f32[1,4,7168]{2,1,0:T(4,128)} %param.11) | copy-start | bytes 344068
  13.4 2.7 %copy-start.2 = (f32[1,4,7168]{2,1,0:T(4,128)S(1)}, f32[1,4,7168]{2,1,0:T(4,128)}, u32[]{:S(2)}) copy-start(f32[1,4,7168]{2,1,0:T(4,128)} %param.12) | copy-start | bytes 344068
  13.4 2.7 %copy-start.3 = (f32[1,4,7168]{2,1,0:T(4,128)S(1)}, f32[1,4,7168]{2,1,0:T(4,128)}, u32[]{:S(2)}) copy-start(f32[1,4,7168]{2,1,0:T(4,128)} %param.13) | copy-start | bytes 344068
  34.2 22.2 %all-to-all-start.2 = ((bf16[32,7,128]{2,1,0:T(8,128)(2,1)}), bf16[32,7,128]{2,1,0:T(8,128)(2,1)S(1)}, u32[]{:S(2)}, u32[]{:S(2)}) async-start(bf16[32,7,128]{2,1,0:T(8,128)(2,1)} %copy.47), calls=%async_computation.2 | async-start | bytes 131072 | tf_op jit(solution)/shard_map/all_to_all | solution.py:104
  50.8 5.7 %copy-start.4 = (f32[896]{0:T(1024)S(1)}, f32[896]{0:T(1024)}, u32[]{:S(2)}) copy-start(f32[896]{0:T(1024)} %param.15) | copy-start | bytes 10756
  50.8 5.7 %copy-start.5 = (f32[896]{0:T(1024)S(1)}, f32[896]{0:T(1024)}, u32[]{:S(2)}) copy-start(f32[896]{0:T(1024)} %param.16) | copy-start | bytes 10756
  50.8 5.7 %copy-start.6 = (f32[896]{0:T(1024)S(1)}, f32[896]{0:T(1024)}, u32[]{:S(2)}) copy-start(f32[896]{0:T(1024)} %param.17) | copy-start | bytes 10756
